TPU v7x, 128 devices: a whole 4x4x4 slice. The times are simulated.
128 devices in a mesh: rows: 16 (over x, y), cols: 8 (over z, core).
Axes of the slice: x: 4, y: 4, z: 4, core: 2. Of those that a mesh axis runs over, the one named last changes fastest.
Arguments:
- coarse: float32 [1024, 1024], P('rows', 'cols'), may hold values from -6 to 6
- detail4: float32 [3, 1024, 1024], P(None, 'rows', 'cols'), may hold values from -6 to 6
- detail3: float32 [3, 2048, 2048], P(None, 'rows', 'cols'), may hold values from -6 to 6
- detail2: float32 [3, 4096, 4096], P(None, 'rows', 'cols'), may hold values from -6 to 6
- detail1: float32 [3, 8192, 8192], P(None, 'rows', 'cols'), may hold values from -6 to 6
Outputs:
- image: float32 [16384, 16384], P('rows', 'cols')
All inputs are finite; a program needn't handle non-finite values.
Results may differ from a plain program's by a relative error of at most 0.00013.
Values sent between devices are 32-bit elements; how exact they have to be, the bound alone decides.
No kernel may reach another device: no remote copies, remote signals or barrier semaphores. Data moves between devices by JAX's collectives and lax.ppermute only.
A program may use at most 128 MiB of HBM per device.

v0:
```python
import functools

import jax
import jax.numpy as jnp
from jax import lax
from jax.experimental import pallas as pl
from jax.experimental.pallas import tpu as pltpu
from jax.sharding import PartitionSpec as P

lift_alpha = -1.586134342059924
lift_beta = -0.052980118572961
lift_gamma = 0.882911075530934
lift_delta = 0.443506852043971
lift_scale = 1.149604398860241
SQ = lift_scale * lift_scale

H = (512, 256, 128, 64)
W = (1024, 512, 256, 128)
PLANES = tuple((k, p) for k in range(4) for p in range(3)) + ((3, 3),)
ROFF = []
COFF = []
_r = _c = 0
for _k, _p in PLANES:
    ROFF.append(_r)
    COFF.append(_c)
    _r += W[_k]
    _c += H[_k] // 8 + 1
RW = _r
CG = _c
HALF = RW // 2
PK = -(-CG // 32)

f32 = jnp.float32
bf16 = jnp.bfloat16


def iota(shape, dim):
    return lax.broadcasted_iota(jnp.int32, shape, dim)


def row_pack_kernel(*refs):
    tops, bots = refs[0:5], refs[5:10]
    up, down = refs[10], refs[11]
    top, bot = [], []
    for k, p in PLANES:
        if p == 3:
            top.append(tops[4][...])
            bot.append(bots[4][...])
        else:
            top.append(tops[k][p])
            bot.append(bots[k][p])
    top = jnp.concatenate(top, axis=1)
    bot = jnp.concatenate(bot, axis=1)
    low = iota((8, HALF), 0) < 4
    up[...] = jnp.where(low, top[:, :HALF], pltpu.roll(top[:, HALF:], 4, 0))
    down[...] = jnp.where(low, pltpu.roll(bot[:, :HALF], 4, 0), bot[:, HALF:])


def row_pack(coarse, details):
    def spec(k, last):
        row = H[k] // 8 - 1 if last else 0
        return pl.BlockSpec((3, 8, W[k]), lambda i: (0, row, 0))

    def cspec(last):
        row = H[3] // 8 - 1 if last else 0
        return pl.BlockSpec((8, W[3]), lambda i: (row, 0))

    specs = [spec(k, False) for k in range(4)] + [cspec(False)]
    specs += [spec(k, True) for k in range(4)] + [cspec(True)]
    out = jax.ShapeDtypeStruct((8, HALF), f32)
    return pl.pallas_call(
        row_pack_kernel,
        grid=(1,),
        in_specs=specs,
        out_specs=[pl.BlockSpec((8, HALF), lambda i: (0, 0))] * 2,
        out_shape=[out, out],
        name="row_pack",
    )(*details, coarse, *details, coarse)


def row_unpack(after, before):
    low = iota(after.shape, 0) < 4
    first = jnp.where(low, after, pltpu.roll(before, 4, 0))
    second = jnp.where(low, pltpu.roll(after, 4, 0), before)
    return first, second


def col_pack_kernel(*refs):
    lefts, rights = refs[0:5], refs[5:10]
    after, before = refs[10], refs[11]
    left_out, right_out = refs[12], refs[13]
    first, second = row_unpack(after[...], before[...])
    ext = jnp.concatenate([first, second], axis=1)
    lane = iota((8, 128), 1)

    def edge(q):
        n = max(i for i in range(13) if COFF[i] <= q)
        k, p = PLANES[n]
        g = q - COFF[n]
        if g == H[k] // 8:
            o = ROFF[n]
            lo, hi = ext[:, o : o + 128], ext[:, o + W[k] - 128 : o + W[k]]
        elif p == 3:
            lo, hi = lefts[4][8 * g : 8 * g + 8, :], rights[4][8 * g : 8 * g + 8, :]
        else:
            lo, hi = lefts[k][p, 8 * g : 8 * g + 8, :], rights[k][p, 8 * g : 8 * g + 8, :]
        return jnp.where(lane < 64, lo, hi)

    lacc = [jnp.zeros((8, 128), f32) for _ in range(PK)]
    racc = [jnp.zeros((8, 128), f32) for _ in range(PK)]
    for j in range(32):
        start = 4 * j
        nxt = (4 * j + 4) % 128
        rmask = (lane >= start) & (lane < start + 4)
        lmask = (lane >= nxt) & (lane < nxt + 4)
        for m in range(PK):
            q = 32 * m + j
            if q < CG:
                e = edge(q)
                if nxt:
                    e = pltpu.roll(e, nxt, 1)
                lacc[m] = jnp.where(lmask, e, lacc[m])
                racc[m] = jnp.where(rmask, e, racc[m])
    for m in range(PK):
        left_out[8 * m : 8 * m + 8, :] = lacc[m]
        right_out[8 * m : 8 * m + 8, :] = racc[m]


def col_pack(coarse, details, after, before):
    def spec(k, last):
        col = W[k] // 128 - 1 if last else 0
        return pl.BlockSpec((3, H[k], 128), lambda i: (0, 0, col))

    def cspec(last):
        col = W[3] // 128 - 1 if last else 0
        return pl.BlockSpec((H[3], 128), lambda i: (0, col))

    specs = [spec(k, False) for k in range(4)] + [cspec(False)]
    specs += [spec(k, True) for k in range(4)] + [cspec(True)]
    specs += [pl.BlockSpec((8, HALF), lambda i: (0, 0))] * 2
    out = jax.ShapeDtypeStruct((8 * PK, 128), f32)
    return pl.pallas_call(
        col_pack_kernel,
        grid=(1,),
        in_specs=specs,
        out_specs=[pl.BlockSpec((8 * PK, 128), lambda i: (0, 0))] * 2,
        out_shape=[out, out],
        name="col_pack",
    )(*details, coarse, *details, coarse, after, before)


def vertical(load_s, load_r, groups, store_s, store_r):
    sub = iota((8, 128), 0)
    first, last = sub == 0, sub == 7
    memo = {}

    def cached(f):
        def get(g):
            g = g % groups
            if (f, g) not in memo:
                memo[(f, g)] = f(g)
            return memo[(f, g)]

        return get

    s = cached(lambda g: load_s(g))
    r = cached(lambda g: load_r(g))

    def prev_of(x):
        turned = cached(lambda g: pltpu.roll(x(g), 1, 0))
        return lambda g: jnp.where(first, turned(g - 1), turned(g))

    def next_of(x):
        turned = cached(lambda g: pltpu.roll(x(g), 7, 0))
        return lambda g: jnp.where(last, turned(g + 1), turned(g))

    rp = prev_of(r)
    s1 = cached(lambda g: s(g) - lift_delta * (r(g) + rp(g)))
    s1n = next_of(s1)
    r1 = cached(lambda g: r(g) - lift_gamma * (s1(g) + s1n(g)))
    r1p = prev_of(r1)
    s2 = cached(lambda g: s1(g) - lift_beta * (r1(g) + r1p(g)))
    s2n = next_of(s2)
    r2 = cached(lambda g: r1(g) - lift_alpha * (s2(g) + s2n(g)))
    for g in range(groups):
        store_s(g, s2(g))
        store_r(g, r2(g))


def horizontal(s, r):
    n = s.shape[1]
    s = s - lift_delta * (r + pltpu.roll(r, 1, 1))
    r = r - lift_gamma * (s + pltpu.roll(s, n - 1, 1))
    s = s - lift_beta * (r + pltpu.roll(r, 1, 1))
    r = r - lift_alpha * (s + pltpu.roll(s, n - 1, 1))
    return s, r


def interleave(s, r, blocks, perm):
    rows = s.shape[0]
    x = jnp.concatenate(
        [
            jnp.concatenate([s[:, 128 * b : 128 * b + 128], r[:, 128 * b : 128 * b + 128]], axis=1)
            for b in range(blocks)
        ],
        axis=0,
    )
    hi = x.astype(bf16)
    lo = (x - hi.astype(f32)).astype(bf16)
    y = jnp.dot(jnp.concatenate([hi, lo], axis=1), perm, preferred_element_type=f32)
    return [y[rows * b : rows * b + rows, :] for b in range(blocks)]


ROWS = 64
SLOTS = 4


def main_kernel(
    coarse, d4, d3, d2, d1, rafter, rbefore, cafter, cbefore, out,
    xr, xc, u, v, l3, l2, l1, perm, stage, sems,
):
    details = (d1, d2, d3, d4)
    lows = (l1, l2, l3)
    lane = iota((8, 128), 1)
    first, second = row_unpack(rafter[...], rbefore[...])
    xr[:, :HALF] = first
    xr[:, HALF:] = second

    even = (iota((8 * PK, 128), 1) % 8) < 4
    aft, bef = cafter[...], cbefore[...]
    comb = (jnp.where(even, bef, aft), jnp.where(even, aft, bef))
    keep = (lane < 4) | (lane >= 124)
    for q in range(CG):
        m, j = divmod(q, 32)
        t = comb[j % 2][8 * m : 8 * m + 8, :]
        shift = (124 - 4 * j) % 128
        if shift:
            t = pltpu.roll(t, shift, 1)
        xc[8 * q : 8 * q + 8, :] = jnp.where(keep, t, 0.0)

    row = iota((512, 256), 0) % 256
    col = iota((512, 256), 1)
    target = jnp.where(row < 128, 2 * row, 2 * row - 255)
    perm[...] = jnp.where(col == target, 1.0, 0.0).astype(bf16)

    for k in (3, 2, 1, 0):
        h, w = H[k], W[k]
        groups, blocks = h // 8 + 1, w // 128

        def load(p, g, b, k=k, h=h, w=w, groups=groups, blocks=blocks):
            static = isinstance(b, int)
            n = 3 * k + p if p < 3 else 12
            if p == 3 and k < 3:
                at = 128 * b if static else pl.multiple_of(b * 128, 128)
                return lows[k][8 * g : 8 * g + 8, pl.ds(at, 128)]
            if static and b == blocks:
                q = COFF[n] + g
                return xc[8 * q : 8 * q + 8, :]
            if g == groups - 1:
                at = ROFF[n] + 128 * b
                if not static:
                    at = pl.multiple_of(at, 128)
                return xr[:, pl.ds(at, 128)]
            at = 128 * b if static else pl.multiple_of(b * 128, 128)
            if p == 3:
                return coarse[8 * g : 8 * g + 8, pl.ds(at, 128)]
            return details[k][p, 8 * g : 8 * g + 8, pl.ds(at, 128)]

        def columns(b, load=load, groups=groups, k=k):
            def store(ref, odd):
                def put(g, x):
                    if k == 0 and g == groups - 1:
                        return
                    ref[b, pl.ds(16 * g + odd, 8, 2), :] = x

                return put

            vertical(
                lambda g: load(3, g, b) * SQ, lambda g: load(1, g, b), groups, store(u, 0), store(u, 1)
            )
            vertical(
                lambda g: load(0, g, b), lambda g: load(2, g, b) * (1.0 / SQ), groups, store(v, 0), store(v, 1)
            )

        if blocks > 1:
            def body(b, c, columns=columns):
                columns(b)
                return c

            lax.fori_loop(0, blocks, body, 0)
        else:
            columns(0)
        columns(blocks)

        def rows_of(at, rows, blocks=blocks):
            s = jnp.concatenate([u[b, pl.ds(at, rows), :] for b in range(blocks + 1)], axis=1)
            r = jnp.concatenate([v[b, pl.ds(at, rows), :] for b in range(blocks + 1)], axis=1)
            return horizontal(s, r)

        if k:
            low = lows[k - 1]
            total = 16 * groups
            rows = {3: 144, 2: 136, 1: 88}[k]

            def chunk(i, c, rows=rows, rows_of=rows_of, low=low, blocks=blocks):
                at = pl.multiple_of(i * rows, 8)
                s, r = rows_of(at, rows)
                parts = interleave(s, r, blocks + 1, perm[...])
                for b in range(blocks):
                    low[pl.ds(at, rows), 256 * b : 256 * b + 256] = parts[b]
                left, right = parts[blocks][:, :128], parts[blocks][:, 128:]
                low[pl.ds(at, rows), 256 * blocks : 256 * blocks + 128] = jnp.where(
                    iota((rows, 128), 1) < 64, left, right
                )
                return c

            lax.fori_loop(0, total // rows, chunk, 0)
            top = low[2 * h : 2 * h + 8, :]
            bottom = low[2 * h + 8 : 2 * h + 16, :]
            low[2 * h : 2 * h + 8, :] = jnp.where(iota(top.shape, 0) < 4, top, bottom)
        else:
            def copy(i, slot):
                return pltpu.make_async_copy(
                    stage.at[slot], out.at[pl.ds(pl.multiple_of(i * ROWS, 8), ROWS), :], sems.at[slot]
                )

            def chunk(i, c, rows_of=rows_of, blocks=blocks):
                slot = lax.rem(i, SLOTS)

                @pl.when(i >= SLOTS)
                def _():
                    copy(i - SLOTS, slot).wait()

                s, r = rows_of(pl.multiple_of(i * ROWS, 8), ROWS)
                parts = interleave(s, r, blocks, perm[...])
                for b in range(blocks):
                    stage[slot, :, 256 * b : 256 * b + 256] = parts[b]
                copy(i, slot).start()
                return c

            n = 2 * h // ROWS
            lax.fori_loop(0, n, chunk, 0)
            for i in range(n - SLOTS, n):
                copy(i, i % SLOTS).wait()


def main(coarse, d4, d3, d2, d1, rafter, rbefore, cafter, cbefore):
    vmem = pl.BlockSpec(memory_space=pltpu.VMEM)
    return pl.pallas_call(
        main_kernel,
        in_specs=[vmem] * 9,
        out_specs=pl.BlockSpec(memory_space=pl.ANY),
        out_shape=jax.ShapeDtypeStruct((1024, 2048), f32),
        scratch_shapes=[
            pltpu.VMEM((8, RW), f32),
            pltpu.VMEM((8 * CG, 128), f32),
            pltpu.VMEM((9, 1040, 128), f32),
            pltpu.VMEM((9, 1040, 128), f32),
            pltpu.VMEM((144, 384), f32),
            pltpu.VMEM((272, 640), f32),
            pltpu.VMEM((528, 1152), f32),
            pltpu.VMEM((512, 256), bf16),
            pltpu.VMEM((SLOTS, ROWS, 2048), f32),
            pltpu.SemaphoreType.DMA((SLOTS,)),
        ],
        compiler_params=pltpu.CompilerParams(vmem_limit_bytes=40 << 20),
        name="synthesis",
    )(coarse, d4, d3, d2, d1, rafter, rbefore, cafter, cbefore)


def per_device(coarse, detail4, detail3, detail2, detail1):
    details = (detail1, detail2, detail3, detail4)

    def swap(to_prev, to_next, axis):
        n = lax.axis_size(axis)
        down = [((i + 1) % n, i) for i in range(n)]
        up = [(i, (i + 1) % n) for i in range(n)]
        return lax.ppermute(to_prev, axis, down), lax.ppermute(to_next, axis, up)

    rafter, rbefore = swap(*row_pack(coarse, details), "rows")
    cafter, cbefore = swap(*col_pack(coarse, details, rafter, rbefore), "cols")
    return main(coarse, detail4, detail3, detail2, detail1, rafter, rbefore, cafter, cbefore)


def solution(mesh):
    return jax.shard_map(
        per_device,
        mesh=mesh,
        in_specs=(
            P("rows", "cols"),
            P(None, "rows", "cols"),
            P(None, "rows", "cols"),
            P(None, "rows", "cols"),
            P(None, "rows", "cols"),
        ),
        out_specs=P("rows", "cols"),
        check_vma=False,
    )
```

profile of v0, /device:TPU:0, one launch (start us, length us, event | category | flops | bytes accessed | tf_op | source)
XLA Modules:
  0.0 53.0 jit_solution(16133980606044945379)
XLA Ops:
  0.0 1.7 %row_pack.1 = (f32[8,2944]{1,0:T(8,128)}, f32[8,2944]{1,0:T(8,128)}) custom-call(f32[3,512,1024]{2,1,0:T(8,128)} %d1.1, f32[3,256,512]{2,1,0:T(8,128)} %d2.1, f32[3,128,256]{2,1,0:T(8,128)} %d3.1, f32[3,64,128]{2,1,0:T(8,128)} %d4.1, f32[64,128]{1,0:T(8,128)} %coarse.1, f32[3,512,1024]{2,1,0:T(8,128)} %d1.1, f32[3,256,512]{2,1,0:T(8,128)} %d2.1, ...), custom_call_target="tpu_custom_call" | custom-call | tf_op jit(solution)/shard_map/row_pack/pallas_call | solution.py:71
  1.7 5.3 %collective-permute-start = (f32[8,2944]{1,0:T(8,128)}, f32[8,2944]{1,0:T(8,128)S(1)}, u32[]{:S(2)}, u32[]{:S(2)}) collective-permute-start(f32[8,2944]{1,0:T(8,128)} %get-tuple-element.9), channel_id=1, source_target_pairs={{8,0},{16,8},{24,16},{32,24},{40,32},{48,40},{56,48},{64,56},{72,6... | collective-permute-start | bytes 282632 | tf_op jit(solution)/shard_map/ppermute | solution.py:378
  7.0 0.0 copy-start.1
  7.0 0.0 copy-start.2
  7.0 0.0 copy-start.3
  7.0 0.0 copy-start.4
  7.0 0.1 collective-permute-start.1
  7.1 2.4 %collective-permute-done.refs_10_.rafter = f32[8,2944]{1,0:T(8,128)S(1)} collective-permute-done((f32[8,2944]{1,0:T(8,128)}, f32[8,2944]{1,0:T(8,128)S(1)}, u32[]{:S(2)}, u32[]{:S(2)}) %collective-permute-start) | collective-permute-done | bytes 94240 | tf_op jit(solution)/shard_map/ppermute | solution.py:378
  9.5 0.0 copy-start.5
  9.5 5.7 %collective-permute-done.1.refs_11_.rbefore = f32[8,2944]{1,0:T(8,128)S(1)} collective-permute-done((f32[8,2944]{1,0:T(8,128)}, f32[8,2944]{1,0:T(8,128)S(1)}, u32[]{:S(2)}, u32[]{:S(2)}) %collective-permute-start.1) | collective-permute-done | bytes 94240 | tf_op jit(solution)/shard_map/ppermute | solution.py:378
  15.2 0.0 copy-done.5
  15.2 0.0 copy-start.7
  15.2 0.6 %copy-done.7 = f32[8,2944]{1,0:T(8,128)} copy-done((f32[8,2944]{1,0:T(8,128)}, f32[8,2944]{1,0:T(8,128)S(1)}, u32[]{:S(2)}) %copy-start.7) | copy-done | bytes 94232
  15.8 3.0 %col_pack.1 = (f32[96,128]{1,0:T(8,128)}, f32[96,128]{1,0:T(8,128)}) custom-call(f32[3,512,1024]{2,1,0:T(8,128)} %d1.1, f32[3,256,512]{2,1,0:T(8,128)} %d2.1, f32[3,128,256]{2,1,0:T(8,128)} %d3.1, f32[3,64,128]{2,1,0:T(8,128)} %d4.1, f32[64,128]{1,0:T(8,128)} %coarse.1, f32[3,512,1024]{2,1,0:T(8,128)} %d1.1, f32[3,256,512]{2,1,0:T(8,128)} %d2.1, ...), custom_call_target="tpu_custom_call" | custom-call | tf_op jit(solution)/shard_map/col_pack/pallas_call | solution.py:142
  18.8 2.0 %collective-permute-start.2 = (f32[96,128]{1,0:T(8,128)}, f32[96,128]{1,0:T(8,128)S(1)}, u32[]{:S(2)}, u32[]{:S(2)}) collective-permute-start(f32[96,128]{1,0:T(8,128)} %get-tuple-element.11), channel_id=1, source_target_pairs={{1,0},{2,1},{3,2},{4,3},{5,4},{6,5},{7,6},{0,7},{9,8},{10,9},{11,1... | collective-permute-start | bytes 147464 | tf_op jit(solution)/shard_map/ppermute | solution.py:378
  20.9 0.0 collective-permute-start.3
  20.9 2.1 %collective-permute-done.2.cafter = f32[96,128]{1,0:T(8,128)S(1)} collective-permute-done((f32[96,128]{1,0:T(8,128)}, f32[96,128]{1,0:T(8,128)S(1)}, u32[]{:S(2)}, u32[]{:S(2)}) %collective-permute-start.2) | collective-permute-done | bytes 49184 | tf_op jit(solution)/shard_map/ppermute | solution.py:378
  22.9 2.9 %collective-permute-done.3.cbefore = f32[96,128]{1,0:T(8,128)S(1)} collective-permute-done((f32[96,128]{1,0:T(8,128)}, f32[96,128]{1,0:T(8,128)S(1)}, u32[]{:S(2)}, u32[]{:S(2)}) %collective-permute-start.3) | collective-permute-done | bytes 49184 | tf_op jit(solution)/shard_map/ppermute | solution.py:378
  25.8 0.0 copy-done.1
  25.8 0.0 copy-done.2
  25.8 0.0 copy-done.3
  25.8 0.0 copy-done.4
  25.8 0.0 copy-start
  25.9 2.8 %copy-done = f32[3,512,1024]{2,1,0:T(8,128)S(1)} copy-done((f32[3,512,1024]{2,1,0:T(8,128)S(1)}, f32[3,512,1024]{2,1,0:T(8,128)}, u32[]{:S(2)}) %copy-start) | copy-done | bytes 6291480
  28.6 0.0 copy-start.6
  28.6 0.9 %copy-done.6 = f32[8,2944]{1,0:T(8,128)S(1)} copy-done((f32[8,2944]{1,0:T(8,128)S(1)}, f32[8,2944]{1,0:T(8,128)}, u32[]{:S(2)}) %copy-start.6) | copy-done | bytes 94232
  29.5 0.0 copy-start.8
  29.5 0.9 %copy-done.8 = f32[8,2944]{1,0:T(8,128)S(1)} copy-done((f32[8,2944]{1,0:T(8,128)S(1)}, f32[8,2944]{1,0:T(8,128)}, u32[]{:S(2)}) %copy-start.8) | copy-done | bytes 94232
  30.4 22.6 %synthesis.1 = f32[1024,2048]{1,0:T(8,128)} custom-call(f32[64,128]{1,0:T(8,128)S(1)} %copy-done.4, f32[3,64,128]{2,1,0:T(8,128)S(1)} %copy-done.3, f32[3,128,256]{2,1,0:T(8,128)S(1)} %copy-done.2, f32[3,256,512]{2,1,0:T(8,128)S(1)} %copy-done.1, f32[3,512,1024]{2,1,0:T(8,128)S(1)} %copy-done, f32[8,2944]{1,0:T(8,128)S(1)} %copy-done.6, ...), custom_call_target="tpu_custom_call" | custom-call | tf_op jit(solution)/shard_map/synthesis/pallas_call | solution.py:349
Async XLA Ops:
  1.7 7.8 %collective-permute-start = (f32[8,2944]{1,0:T(8,128)}, f32[8,2944]{1,0:T(8,128)S(1)}, u32[]{:S(2)}, u32[]{:S(2)}) collective-permute-start(f32[8,2944]{1,0:T(8,128)} %get-tuple-element.9), channel_id=1, source_target_pairs={{8,0},{16,8},{24,16},{32,24},{40,32},{48,40},{56,48},{64,56},{72,6... | collective-permute-start | bytes 282632 | tf_op jit(solution)/shard_map/ppermute | solution.py:378
  7.0 18.8 %copy-start.1 = (f32[3,256,512]{2,1,0:T(8,128)S(1)}, f32[3,256,512]{2,1,0:T(8,128)}, u32[]{:S(2)}) copy-start(f32[3,256,512]{2,1,0:T(8,128)} %d2.1) | copy-start | bytes 4718596
  7.0 18.8 %copy-start.2 = (f32[3,128,256]{2,1,0:T(8,128)S(1)}, f32[3,128,256]{2,1,0:T(8,128)}, u32[]{:S(2)}) copy-start(f32[3,128,256]{2,1,0:T(8,128)} %d3.1) | copy-start | bytes 1179652
  7.0 18.8 %copy-start.3 = (f32[3,64,128]{2,1,0:T(8,128)S(1)}, f32[3,64,128]{2,1,0:T(8,128)}, u32[]{:S(2)}) copy-start(f32[3,64,128]{2,1,0:T(8,128)} %d4.1) | copy-start | bytes 294916
  7.0 18.8 %copy-start.4 = (f32[64,128]{1,0:T(8,128)S(1)}, f32[64,128]{1,0:T(8,128)}, u32[]{:S(2)}) copy-start(f32[64,128]{1,0:T(8,128)} %coarse.1) | copy-start | bytes 98308
  7.0 8.2 %collective-permute-start.1 = (f32[8,2944]{1,0:T(8,128)}, f32[8,2944]{1,0:T(8,128)S(1)}, u32[]{:S(2)}, u32[]{:S(2)}) collective-permute-start(f32[8,2944]{1,0:T(8,128)} %get-tuple-element.10), channel_id=1, source_target_pairs={{0,8},{8,16},{16,24},{24,32},{32,40},{40,48},{48,56},{56,64},{64,7... | collective-permute-start | bytes 282632 | tf_op jit(solution)/shard_map/ppermute | solution.py:378
  9.5 5.7 %copy-start.5 = (f32[8,2944]{1,0:T(8,128)}, f32[8,2944]{1,0:T(8,128)S(1)}, u32[]{:S(2)}) copy-start(f32[8,2944]{1,0:T(8,128)S(1)} %collective-permute-done.refs_10_.rafter) | copy-start | bytes 282628
  15.2 0.6 %copy-start.7 = (f32[8,2944]{1,0:T(8,128)}, f32[8,2944]{1,0:T(8,128)S(1)}, u32[]{:S(2)}) copy-start(f32[8,2944]{1,0:T(8,128)S(1)} %collective-permute-done.1.refs_11_.rbefore) | copy-start | bytes 282628
  18.8 4.1 %collective-permute-start.2 = (f32[96,128]{1,0:T(8,128)}, f32[96,128]{1,0:T(8,128)S(1)}, u32[]{:S(2)}, u32[]{:S(2)}) collective-permute-start(f32[96,128]{1,0:T(8,128)} %get-tuple-element.11), channel_id=1, source_target_pairs={{1,0},{2,1},{3,2},{4,3},{5,4},{6,5},{7,6},{0,7},{9,8},{10,9},{11,1... | collective-permute-start | bytes 147464 | tf_op jit(solution)/shard_map/ppermute | solution.py:378
  20.9 4.9 %collective-permute-start.3 = (f32[96,128]{1,0:T(8,128)}, f32[96,128]{1,0:T(8,128)S(1)}, u32[]{:S(2)}, u32[]{:S(2)}) collective-permute-start(f32[96,128]{1,0:T(8,128)} %get-tuple-element.12), channel_id=1, source_target_pairs={{0,1},{1,2},{2,3},{3,4},{4,5},{5,6},{6,7},{7,0},{8,9},{9,10},{10,1... | collective-permute-start | bytes 147464 | tf_op jit(solution)/shard_map/ppermute | solution.py:378
  25.8 2.8 %copy-start = (f32[3,512,1024]{2,1,0:T(8,128)S(1)}, f32[3,512,1024]{2,1,0:T(8,128)}, u32[]{:S(2)}) copy-start(f32[3,512,1024]{2,1,0:T(8,128)} %d1.1) | copy-start | bytes 18874372
  28.6 0.9 %copy-start.6 = (f32[8,2944]{1,0:T(8,128)S(1)}, f32[8,2944]{1,0:T(8,128)}, u32[]{:S(2)}) copy-start(f32[8,2944]{1,0:T(8,128)} %copy-done.5) | copy-start | bytes 282628
  29.5 0.9 %copy-start.8 = (f32[8,2944]{1,0:T(8,128)S(1)}, f32[8,2944]{1,0:T(8,128)}, u32[]{:S(2)}) copy-start(f32[8,2944]{1,0:T(8,128)} %copy-done.7) | copy-start | bytes 282628
where the time goes:
time: 53.3 us; the launch traced here: 53 us
  Pallas kernels  27.3 us (51%)
  waiting for transfers between devices  13 us (24%)
  starting transfers between devices  7.44 us (14%)
  local copies, waits for them, and re-layouts  5.21 us (10%)
    pallas_call x1, Pallas kernels, main(): pl.pallas_call(main_kernel, in_specs=[vmem] * 9, out_specs=pl.BlockSpec(m...  22.6 us
    ppermute x4, waiting for transfers between devices, swap(): return (lax.ppermute(to_prev, axis, down), lax.ppermute(to_next, axis, up))  13 us
    ppermute x4, starting transfers between devices, swap(): return (lax.ppermute(to_prev, axis, down), lax.ppermute(to_next, axis, up))  7.44 us
    unnamed x18, local copies, waits for them, and re-layouts  5.21 us
    pallas_call x1, Pallas kernels, col_pack(): pl.pallas_call(col_pack_kernel, grid=(1,), in_specs=specs, out_specs=[pl....  3.01 us
    pallas_call x1, Pallas kernels, row_pack(): pl.pallas_call(row_pack_kernel, grid=(1,), in_specs=specs, out_specs=[pl....  1.69 us
  transfers between devices with their start and end apart: 4, of which 4 were waited for; matrix products, arithmetic and copies ran while one was open for 0% of the time, Pallas kernels for 0%

commit v1 on v0

v1 whole, which is shorter than its diff:
```python
import functools

import jax
import jax.numpy as jnp
from jax import lax
from jax.experimental import pallas as pl
from jax.experimental.pallas import tpu as pltpu
from jax.sharding import PartitionSpec as P

lift_alpha = -1.586134342059924
lift_beta = -0.052980118572961
lift_gamma = 0.882911075530934
lift_delta = 0.443506852043971
lift_scale = 1.149604398860241
SQ = lift_scale * lift_scale

H = (512, 256, 128, 64)
W = (1024, 512, 256, 128)
PLANES = tuple((k, p) for k in range(4) for p in range(3)) + ((3, 3),)
ROFF = []
COFF = []
_r = _c = 0
for _k, _p in PLANES:
    ROFF.append(_r)
    COFF.append(_c)
    _r += W[_k]
    _c += H[_k] // 8
RW = _r
OWN = _c
CG = OWN + 13
HALF = RW // 2
PK = -(-CG // 32)
CORNER = OWN // 32

f32 = jnp.float32
bf16 = jnp.bfloat16
VMEM = pl.BlockSpec(memory_space=pltpu.VMEM)
HBM = pl.BlockSpec(memory_space=pltpu.HBM)
SMALL = pltpu.CompilerParams(vmem_limit_bytes=6 << 20)


def iota(shape, dim):
    return lax.broadcasted_iota(jnp.int32, shape, dim)


def col_group(n, g):
    return OWN + n if g == H[PLANES[n][0]] // 8 else COFF[n] + g


def row_pack_kernel(d1, d2, d3, d4, coarse, up, down, top, bot, sems):
    copies = []
    for n, (k, p) in enumerate(PLANES):
        src = coarse if p == 3 else (d1, d2, d3, d4)[k].at[p]
        lanes = pl.ds(ROFF[n], W[k])
        copies.append(pltpu.make_async_copy(src.at[pl.ds(0, 8), :], top.at[:, lanes], sems.at[2 * n]))
        copies.append(
            pltpu.make_async_copy(src.at[pl.ds(H[k] - 8, 8), :], bot.at[:, lanes], sems.at[2 * n + 1])
        )
    for c in copies:
        c.start()
    for c in copies:
        c.wait()
    low = iota((8, HALF), 0) < 4
    up[...] = jnp.where(low, top[:, :HALF], pltpu.roll(top[:, HALF:], 4, 0))
    down[...] = jnp.where(low, pltpu.roll(bot[:, :HALF], 4, 0), bot[:, HALF:])


def row_pack(coarse, details):
    out = jax.ShapeDtypeStruct((8, HALF), f32)
    return pl.pallas_call(
        row_pack_kernel,
        in_specs=[HBM] * 5,
        out_specs=[VMEM] * 2,
        out_shape=[out, out],
        scratch_shapes=[
            pltpu.VMEM((8, RW), f32),
            pltpu.VMEM((8, RW), f32),
            pltpu.SemaphoreType.DMA((26,)),
        ],
        compiler_params=SMALL,
        name="row_pack",
    )(*(pltpu.with_memory_space_constraint(x, pltpu.HBM) for x in (*details, coarse)))


def row_unpack(after, before):
    low = iota(after.shape, 0) < 4
    first = jnp.where(low, after, pltpu.roll(before, 4, 0))
    second = jnp.where(low, pltpu.roll(after, 4, 0), before)
    return first, second


def place(edges, lacc, racc):
    lane = iota((8, 128), 1)
    for q, e in edges:
        m, j = divmod(q, 32)
        nxt = (4 * j + 4) % 128
        e = e()
        if nxt:
            e = pltpu.roll(e, nxt, 1)
        lacc[m] = jnp.where((lane >= nxt) & (lane < nxt + 4), e, lacc[m])
        racc[m] = jnp.where((lane >= 4 * j) & (lane < 4 * j + 4), e, racc[m])


def col_pack_kernel(d1, d2, d3, d4, coarse, _, left_out, right_out):
    details = (d1, d2, d3, d4)
    lane = iota((8, 128), 1)

    def edge(n, g):
        k, p = PLANES[n]
        rows = slice(8 * g, 8 * g + 8)
        if p == 3:
            return coarse[rows, :]
        lo, hi = details[k][p, rows, :128], details[k][p, rows, W[k] - 128 :]
        return jnp.where(lane < 64, lo, hi)

    order = {}
    for n, (k, p) in enumerate(PLANES):
        for g in range(H[k] // 8):
            order[COFF[n] + g] = functools.partial(edge, n, g)
    lacc = {m: jnp.zeros((8, 128), f32) for m in range(PK)}
    racc = {m: jnp.zeros((8, 128), f32) for m in range(PK)}
    place([(q, order[q]) for j in range(32) for q in range(j, OWN, 32)], lacc, racc)
    for m in range(PK):
        left_out[8 * m : 8 * m + 8, :] = lacc[m]
        right_out[8 * m : 8 * m + 8, :] = racc[m]


def corner_kernel(left, right, after, before, left_out, right_out):
    first, second = row_unpack(after[...], before[...])
    lane = iota((8, 128), 1)
    left_out[...] = left[...]
    right_out[...] = right[...]

    def piece(o):
        return first[:, o : o + 128] if o < HALF else second[:, o - HALF : o - HALF + 128]

    def edge(n):
        return jnp.where(lane < 64, piece(ROFF[n]), piece(ROFF[n] + W[PLANES[n][0]] - 128))

    rows = slice(8 * CORNER, 8 * CORNER + 8)
    lacc, racc = {CORNER: left[rows, :]}, {CORNER: right[rows, :]}
    place([(OWN + n, functools.partial(edge, n)) for n in range(13)], lacc, racc)
    left_out[rows, :] = lacc[CORNER]
    right_out[rows, :] = racc[CORNER]


def col_pack(coarse, details, after_this):
    out = jax.ShapeDtypeStruct((8 * PK, 128), f32)
    return pl.pallas_call(
        col_pack_kernel,
        in_specs=[VMEM] * 5 + [HBM],
        out_specs=[VMEM] * 2,
        out_shape=[out, out],
        compiler_params=SMALL,
        name="col_pack",
    )(*details, coarse, after_this)


def corners(left, right, after, before):
    out = jax.ShapeDtypeStruct((8 * PK, 128), f32)
    return pl.pallas_call(
        corner_kernel,
        in_specs=[VMEM] * 4,
        out_specs=[VMEM] * 2,
        out_shape=[out, out],
        compiler_params=SMALL,
        name="corners",
    )(left, right, after, before)


def vertical(load_s, load_r, groups, store_s, store_r, tmp):
    sub = iota((8, 128), 0)
    first, last = sub == 0, sub == 7

    def cached(f):
        memo = {}

        def get(g):
            g = g % groups
            if g not in memo:
                memo[g] = f(g)
            return memo[g]

        return get

    def kept(f, ref):
        def make(g):
            x = f(g)
            ref[8 * g : 8 * g + 8, :] = x
            return x

        return cached(make)

    def prev_of(x, ref):
        def get(g):
            a, b = x(g - 1), x(g)
            if g:
                return ref[8 * g - 1 : 8 * g + 7, :]
            return jnp.where(first, pltpu.roll(a, 1, 0), pltpu.roll(b, 1, 0))

        return get

    def next_of(x, ref):
        def get(g):
            a, b = x(g), x(g + 1)
            if g < groups - 1:
                return ref[8 * g + 1 : 8 * g + 9, :]
            return jnp.where(last, pltpu.roll(b, 7, 0), pltpu.roll(a, 7, 0))

        return get

    s = cached(load_s)
    r = kept(load_r, tmp.at[0])
    rp = prev_of(r, tmp.at[0])
    s1 = kept(lambda g: s(g) - lift_delta * (r(g) + rp(g)), tmp.at[1])
    s1n = next_of(s1, tmp.at[1])
    r1 = kept(lambda g: r(g) - lift_gamma * (s1(g) + s1n(g)), tmp.at[2])
    r1p = prev_of(r1, tmp.at[2])
    s2 = kept(lambda g: s1(g) - lift_beta * (r1(g) + r1p(g)), tmp.at[3])
    s2n = next_of(s2, tmp.at[3])
    r2 = cached(lambda g: r1(g) - lift_alpha * (s2(g) + s2n(g)))
    for g in range(groups):
        store_s(g, s2(g))
        store_r(g, r2(g))


def lanes_of(b):
    return pl.ds(128 * b if isinstance(b, int) else pl.multiple_of(b * 128, 128), 128)


def interleaved_store(ref, odd, skip):
    def put(g, x):
        if g != skip:
            ref[pl.ds(16 * g + odd, 8, 2), :] = x

    return put


def high_columns(k, load, ref, tmp):
    groups = H[k] // 8 + 1
    skip = groups - 1 if k == 0 else -1
    vertical(
        lambda g: load(0, g),
        lambda g: load(2, g) * (1.0 / SQ),
        groups,
        interleaved_store(ref, 0, skip),
        interleaved_store(ref, 1, skip),
        tmp,
    )


def loop(n, f):
    if n == 1:
        f(0)
    else:
        lax.fori_loop(0, n, lambda i, c: (f(i), c)[1], 0)


def detail_kernel(d1, d2, d3, d4, after, before, v1, v2, v3, v4, xr, tmp):
    details, vs = (d1, d2, d3, d4), (v1, v2, v3, v4)
    first, second = row_unpack(after[...], before[...])
    xr[:, :HALF] = first
    xr[:, HALF:] = second
    for k in (3, 2, 1, 0):
        def columns(b, k=k):
            def load(p, g):
                if g == H[k] // 8:
                    o = ROFF[3 * k + p]
                    if isinstance(b, int):
                        return xr[:, o + 128 * b : o + 128 * b + 128]
                    return xr[:, pl.ds(pl.multiple_of(o + b * 128, 128), 128)]
                return details[k][p, 8 * g : 8 * g + 8, lanes_of(b)]

            high_columns(k, load, vs[k].at[b], tmp)

        loop(W[k] // 128, columns)


def detail_columns(details, after, before):
    outs = [jax.ShapeDtypeStruct((W[k] // 128, 2 * H[k] + 16, 128), f32) for k in range(4)]
    outs.append(jax.ShapeDtypeStruct((8, RW), f32))
    return pl.pallas_call(
        detail_kernel,
        in_specs=[VMEM] * 6,
        out_specs=[VMEM] * 5,
        out_shape=outs,
        scratch_shapes=[pltpu.VMEM((4, 520, 128), f32)],
        compiler_params=SMALL,
        name="detail_columns",
    )(*details, after, before)


def horizontal(s, r):
    n = s.shape[1]
    s = s - lift_delta * (r + pltpu.roll(r, 1, 1))
    r = r - lift_gamma * (s + pltpu.roll(s, n - 1, 1))
    s = s - lift_beta * (r + pltpu.roll(r, 1, 1))
    r = r - lift_alpha * (s + pltpu.roll(s, n - 1, 1))
    return s, r


def interleave(s, r, blocks, perm):
    rows = s.shape[0]
    x = jnp.concatenate(
        [
            jnp.concatenate([s[:, 128 * b : 128 * b + 128], r[:, 128 * b : 128 * b + 128]], axis=1)
            for b in range(blocks)
        ],
        axis=0,
    )
    hi = x.astype(bf16)
    lo = (x - hi.astype(f32)).astype(bf16)
    y = jnp.dot(jnp.concatenate([hi, lo], axis=1), perm, preferred_element_type=f32)
    return [y[rows * b : rows * b + rows, :] for b in range(blocks)]


CHUNK = (128, 264, 272, 144)
SLOTS = 3


def main_kernel(
    coarse, d4, d3, d2, d1, v1, v2, v3, v4, xr, cafter, cbefore, out,
    xc, u, vx, l3, l2, l1, perm, stage, tmp, sems,
):
    details, vs = (d1, d2, d3, d4), (v1, v2, v3, v4)
    lows = (l1, l2, l3)
    lane = iota((8, 128), 1)

    even = (iota((8 * PK, 128), 1) % 8) < 4
    aft, bef = cafter[...], cbefore[...]
    comb = (jnp.where(even, bef, aft), jnp.where(even, aft, bef))
    keep = (lane < 4) | (lane >= 124)
    for q in range(CG):
        m, j = divmod(q, 32)
        t = comb[j % 2][8 * m : 8 * m + 8, :]
        shift = (124 - 4 * j) % 128
        if shift:
            t = pltpu.roll(t, shift, 1)
        xc[8 * q : 8 * q + 8, :] = jnp.where(keep, t, 0.0)

    row = iota((512, 256), 0) % 256
    col = iota((512, 256), 1)
    target = jnp.where(row < 128, 2 * row, 2 * row - 255)
    perm[...] = jnp.where(col == target, 1.0, 0.0).astype(bf16)

    for k in (3, 2, 1, 0):
        h, w = H[k], W[k]
        groups, blocks = h // 8 + 1, w // 128
        skip = groups - 1 if k == 0 else -1

        def load(p, g, b, k=k, groups=groups, blocks=blocks):
            n = 3 * k + p if p < 3 else 12
            rows = slice(8 * g, 8 * g + 8)
            if p == 3 and k < 3:
                return lows[k][rows, lanes_of(b)]
            if isinstance(b, int) and b == blocks:
                q = col_group(n, g)
                return xc[8 * q : 8 * q + 8, :]
            if g == groups - 1:
                if isinstance(b, int):
                    return xr[:, ROFF[n] + 128 * b : ROFF[n] + 128 * b + 128]
                return xr[:, pl.ds(pl.multiple_of(ROFF[n] + b * 128, 128), 128)]
            if p == 3:
                return coarse[rows, lanes_of(b)]
            return details[k][p, rows, lanes_of(b)]

        def columns(b, load=load, groups=groups, skip=skip):
            vertical(
                lambda g: load(3, g, b) * SQ,
                lambda g: load(1, g, b),
                groups,
                interleaved_store(u.at[b], 0, skip),
                interleaved_store(u.at[b], 1, skip),
                tmp,
            )

        loop(blocks, columns)
        columns(blocks)
        high_columns(k, lambda p, g, load=load, blocks=blocks: load(p, g, blocks), vx, tmp)

        def rows_of(at, rows, blocks=blocks, k=k):
            at = pl.ds(at, rows)
            s = jnp.concatenate([u[b, at, :] for b in range(blocks + 1)], axis=1)
            r = jnp.concatenate([vs[k][b, at, :] for b in range(blocks)] + [vx[at, :]], axis=1)
            return horizontal(s, r)

        rows = CHUNK[k]
        if k:
            low = lows[k - 1]

            def chunk(i, rows=rows, rows_of=rows_of, low=low, blocks=blocks):
                at = i * rows if isinstance(i, int) else pl.multiple_of(i * rows, 8)
                s, r = rows_of(at, rows)
                parts = interleave(s, r, blocks + 1, perm[...])
                for b in range(blocks):
                    low[pl.ds(at, rows), 256 * b : 256 * b + 256] = parts[b]
                left, right = parts[blocks][:, :128], parts[blocks][:, 128:]
                low[pl.ds(at, rows), 256 * blocks : 256 * blocks + 128] = jnp.where(
                    iota((rows, 128), 1) < 64, left, right
                )

            loop(16 * groups // rows, chunk)
            top = low[2 * h : 2 * h + 8, :]
            bottom = low[2 * h + 8 : 2 * h + 16, :]
            low[2 * h : 2 * h + 8, :] = jnp.where(iota(top.shape, 0) < 4, top, bottom)
        else:
            def copy(i, slot, rows=rows):
                return pltpu.make_async_copy(
                    stage.at[slot], out.at[pl.ds(pl.multiple_of(i * rows, 8), rows), :], sems.at[slot]
                )

            def chunk(i, rows_of=rows_of, blocks=blocks, rows=rows):
                slot = lax.rem(i, SLOTS)

                @pl.when(i >= SLOTS)
                def _():
                    copy(i - SLOTS, slot).wait()

                s, r = rows_of(pl.multiple_of(i * rows, 8), rows)
                parts = interleave(s, r, blocks, perm[...])
                for b in range(blocks):
                    stage[slot, :, 256 * b : 256 * b + 256] = parts[b]
                copy(i, slot).start()

            n = 2 * h // rows
            loop(n, chunk)
            for i in range(n - SLOTS, n):
                copy(i, i % SLOTS).wait()


def main(coarse, d4, d3, d2, d1, *rest):
    return pl.pallas_call(
        main_kernel,
        in_specs=[VMEM] * 12,
        out_specs=HBM,
        out_shape=jax.ShapeDtypeStruct((1024, 2048), f32),
        scratch_shapes=[
            pltpu.VMEM((8 * CG, 128), f32),
            pltpu.VMEM((9, 1040, 128), f32),
            pltpu.VMEM((1040, 128), f32),
            pltpu.VMEM((144, 384), f32),
            pltpu.VMEM((272, 640), f32),
            pltpu.VMEM((528, 1152), f32),
            pltpu.VMEM((512, 256), bf16),
            pltpu.VMEM((SLOTS, CHUNK[0], 2048), f32),
            pltpu.VMEM((4, 520, 128), f32),
            pltpu.SemaphoreType.DMA((SLOTS,)),
        ],
        compiler_params=pltpu.CompilerParams(vmem_limit_bytes=32 << 20),
        name="synthesis",
    )(coarse, d4, d3, d2, d1, *rest)


def per_device(coarse, detail4, detail3, detail2, detail1):
    details = (detail1, detail2, detail3, detail4)

    def swap(to_prev, to_next, axis):
        n = lax.axis_size(axis)
        down = [((i + 1) % n, i) for i in range(n)]
        up = [(i, (i + 1) % n) for i in range(n)]
        return lax.ppermute(to_prev, axis, down), lax.ppermute(to_next, axis, up)

    up, down = row_pack(coarse, details)
    rafter, rbefore = swap(up, down, "rows")
    packed = col_pack(coarse, details, up)
    cafter, cbefore = swap(*corners(*packed, rafter, rbefore), "cols")
    highs = detail_columns(details, rafter, rbefore)
    return main(coarse, detail4, detail3, detail2, detail1, *highs, cafter, cbefore)


def solution(mesh):
    return jax.shard_map(
        per_device,
        mesh=mesh,
        in_specs=(
            P("rows", "cols"),
            P(None, "rows", "cols"),
            P(None, "rows", "cols"),
            P(None, "rows", "cols"),
            P(None, "rows", "cols"),
        ),
        out_specs=P("rows", "cols"),
        check_vma=False,
    )
```

time: 53.3 us -> 33.2 us (0.62)
  waiting for transfers between devices: 13 us -> 4.31 us
  Pallas kernels: 27.3 us -> 20.4 us
  local copies, waits for them, and re-layouts: 5.21 us -> 0.02 us
  starting transfers between devices: 7.44 us -> 8.27 us
    ppermute x4, waiting for transfers between devices: 13 us -> 4.31 us  [swap(): return (lax.ppermute(to_prev, axis, down), lax.ppermute(to_next, axis, up))]
    pallas_call x3 -> x5, Pallas kernels: 27.3 us -> 20.4 us  [the longest x1 16.1 us: main(): pl.pallas_call(main_kernel, in_specs=[VMEM] * 12, out_specs=HBM, out_shap...]
    unnamed x18 -> x10, local copies, waits for them, and re-layouts: 5.21 us -> 0.02 us
    ppermute x4, starting transfers between devices: 7.44 us -> 8.27 us  [swap(): return (lax.ppermute(to_prev, axis, down), lax.ppermute(to_next, axis, up))]
  transfers between devices with their start and end apart: 4 -> 4, of which waited for: 4 -> 2; matrix products, arithmetic and copies ran while one was open for 0% -> 0% of each run, Pallas kernels for 0% -> 9%
where the time goes in v1:
time: 33.2 us; the launch traced here: 33.1 us
  Pallas kernels  20.4 us (61%)
  starting transfers between devices  8.27 us (25%)
  waiting for transfers between devices  4.31 us (13%)
    pallas_call x1, Pallas kernels, main(): pl.pallas_call(main_kernel, in_specs=[VMEM] * 12, out_specs=HBM, out_shap...  16.1 us
    ppermute x4, starting transfers between devices, swap(): return (lax.ppermute(to_prev, axis, down), lax.ppermute(to_next, axis, up))  8.27 us
    ppermute x4, waiting for transfers between devices, swap(): return (lax.ppermute(to_prev, axis, down), lax.ppermute(to_next, axis, up))  4.31 us
    pallas_call x1, Pallas kernels, detail_columns(): pl.pallas_call(detail_kernel, in_specs=[VMEM] * 6, out_specs=[VMEM] * 5,...  2.54 us
    pallas_call x1, Pallas kernels, row_pack(): pl.pallas_call(row_pack_kernel, in_specs=[HBM] * 5, out_specs=[VMEM] * 2,...  1.27 us
  transfers between devices with their start and end apart: 4, of which 2 were waited for; matrix products, arithmetic and copies ran while one was open for 0% of the time, Pallas kernels for 9%

profile of v1, /device:TPU:0, one launch (start us, length us, event | category | flops | bytes accessed | tf_op | source)
XLA Modules:
  0.0 33.1 jit_solution(15273089765448562661)
XLA Ops:
  0.0 0.0 copy-start
  0.0 0.0 copy-start.1
  0.0 0.0 copy-start.2
  0.0 0.0 copy-start.3
  0.0 0.0 copy-start.4
  0.0 1.3 %row_pack.1 = (f32[8,2944]{1,0:T(8,128)S(1)}, f32[8,2944]{1,0:T(8,128)S(1)}) custom-call(f32[3,512,1024]{2,1,0:T(8,128)} %d1.7, f32[3,256,512]{2,1,0:T(8,128)} %d2.7, f32[3,128,256]{2,1,0:T(8,128)} %d3.7, f32[3,64,128]{2,1,0:T(8,128)} %d4.7, f32[64,128]{1,0:T(8,128)} %coarse.5), custom_call_target="tpu_custom_call" | custom-call | tf_op jit(solution)/shard_map/row_pack/pallas_call | solution.py:70
  1.3 1.8 %collective-permute-start.1 = (f32[8,2944]{1,0:T(8,128)S(1)}, f32[8,2944]{1,0:T(8,128)S(1)}, u32[]{:S(2)}, u32[]{:S(2)}) collective-permute-start(f32[8,2944]{1,0:T(8,128)S(1)} %get-tuple-element.17), channel_id=1, source_target_pairs={{0,8},{8,16},{16,24},{24,32},{32,40},{40,48},{48,56},{56,64},{64,7... | collective-permute-start | bytes 282632 | tf_op jit(solution)/shard_map/ppermute | solution.py:461
  3.1 3.7 %collective-permute-start = (f32[8,2944]{1,0:T(8,128)S(1)}, f32[8,2944]{1,0:T(8,128)S(1)}, u32[]{:S(2)}, u32[]{:S(2)}) collective-permute-start(f32[8,2944]{1,0:T(8,128)S(1)} %get-tuple-element.16._), channel_id=1, source_target_pairs={{8,0},{16,8},{24,16},{32,24},{40,32},{48,40},{56,48},{64,56},{72,6... | collective-permute-start | bytes 282632 | tf_op jit(solution)/shard_map/ppermute | solution.py:461
  6.8 0.0 copy-done
  6.8 0.0 copy-done.1
  6.8 0.0 copy-done.2
  6.8 0.0 copy-done.3
  6.8 0.0 copy-done.4
  6.8 0.4 %col_pack.1 = (f32[96,128]{1,0:T(8,128)S(1)}, f32[96,128]{1,0:T(8,128)S(1)}) custom-call(f32[3,512,1024]{2,1,0:T(8,128)S(1)} %copy-done, f32[3,256,512]{2,1,0:T(8,128)S(1)} %copy-done.1, f32[3,128,256]{2,1,0:T(8,128)S(1)} %copy-done.2, f32[3,64,128]{2,1,0:T(8,128)S(1)} %copy-done.3, f32[64,128]{1,0:T(8,128)S(1)} %copy-done.4, f32[8,2944]{1,0:T(8,128)S(1)} %get-tuple-element.16._), custom_call_target="tpu_custom_call" | custom-call | tf_op jit(solution)/shard_map/col_pack/pallas_call | solution.py:149
  7.3 2.1 %collective-permute-done.1.before = f32[8,2944]{1,0:T(8,128)S(1)} collective-permute-done((f32[8,2944]{1,0:T(8,128)S(1)}, f32[8,2944]{1,0:T(8,128)S(1)}, u32[]{:S(2)}, u32[]{:S(2)}) %collective-permute-start.1) | collective-permute-done | bytes 94240 | tf_op jit(solution)/shard_map/ppermute | solution.py:461
  9.4 0.0 collective-permute-done.after
  9.4 0.1 corners.1
  9.5 2.8 %collective-permute-start.2 = (f32[96,128]{1,0:T(8,128)S(1)}, f32[96,128]{1,0:T(8,128)S(1)}, u32[]{:S(2)}, u32[]{:S(2)}) collective-permute-start(f32[96,128]{1,0:T(8,128)S(1)} %get-tuple-element.25), channel_id=1, source_target_pairs={{1,0},{2,1},{3,2},{4,3},{5,4},{6,5},{7,6},{0,7},{9,8},{10,9},{11,1... | collective-permute-start | bytes 147464 | tf_op jit(solution)/shard_map/ppermute | solution.py:461
  12.3 0.0 collective-permute-start.3
  12.3 2.5 %detail_columns.1 = (f32[8,1040,128]{2,1,0:T(8,128)S(1)}, f32[4,528,128]{2,1,0:T(8,128)S(1)}, f32[2,272,128]{2,1,0:T(8,128)S(1)}, f32[1,144,128]{2,1,0:T(8,128)S(1)}, f32[8,5888]{1,0:T(8,128)S(1)}) custom-call(f32[3,512,1024]{2,1,0:T(8,128)S(1)} %copy-done, f32[3,256,512]{2,1,0:T(8,128)S(1)} %copy-done.1, f32[3,128,256]{2,1,0:T(8,128)S(1)} %copy-done.2, ...), custom_call_target="tpu_custom_call" | custom-call | tf_op jit(solution)/shard_map/detail_columns/pallas_call | solution.py:282
  14.8 0.0 collective-permute-done.2.cafter
  14.8 2.2 %collective-permute-done.3.cbefore = f32[96,128]{1,0:T(8,128)S(1)} collective-permute-done((f32[96,128]{1,0:T(8,128)S(1)}, f32[96,128]{1,0:T(8,128)S(1)}, u32[]{:S(2)}, u32[]{:S(2)}) %collective-permute-start.3) | collective-permute-done | bytes 49184 | tf_op jit(solution)/shard_map/ppermute | solution.py:461
  17.0 16.1 %synthesis.1 = f32[1024,2048]{1,0:T(8,128)} custom-call(f32[64,128]{1,0:T(8,128)S(1)} %copy-done.4, f32[3,64,128]{2,1,0:T(8,128)S(1)} %copy-done.3, f32[3,128,256]{2,1,0:T(8,128)S(1)} %copy-done.2, f32[3,256,512]{2,1,0:T(8,128)S(1)} %copy-done.1, f32[3,512,1024]{2,1,0:T(8,128)S(1)} %copy-done, f32[8,1040,128]{2,1,0:T(8,128)S(1)} %get-tuple-element.18.v1, ...), custom_call_target="tpu_custom_call" | custom-call | tf_op jit(solution)/shard_map/synthesis/pallas_call | solution.py:432
Async XLA Ops:
  0.0 6.8 %copy-start = (f32[3,512,1024]{2,1,0:T(8,128)S(1)}, f32[3,512,1024]{2,1,0:T(8,128)}, u32[]{:S(2)}) copy-start(f32[3,512,1024]{2,1,0:T(8,128)} %d1.7) | copy-start | bytes 18874372
  0.0 6.8 %copy-start.1 = (f32[3,256,512]{2,1,0:T(8,128)S(1)}, f32[3,256,512]{2,1,0:T(8,128)}, u32[]{:S(2)}) copy-start(f32[3,256,512]{2,1,0:T(8,128)} %d2.7) | copy-start | bytes 4718596
  0.0 6.8 %copy-start.2 = (f32[3,128,256]{2,1,0:T(8,128)S(1)}, f32[3,128,256]{2,1,0:T(8,128)}, u32[]{:S(2)}) copy-start(f32[3,128,256]{2,1,0:T(8,128)} %d3.7) | copy-start | bytes 1179652
  0.0 6.8 %copy-start.3 = (f32[3,64,128]{2,1,0:T(8,128)S(1)}, f32[3,64,128]{2,1,0:T(8,128)}, u32[]{:S(2)}) copy-start(f32[3,64,128]{2,1,0:T(8,128)} %d4.7) | copy-start | bytes 294916
  0.0 6.8 %copy-start.4 = (f32[64,128]{1,0:T(8,128)S(1)}, f32[64,128]{1,0:T(8,128)}, u32[]{:S(2)}) copy-start(f32[64,128]{1,0:T(8,128)} %coarse.5) | copy-start | bytes 98308
  1.3 8.1 %collective-permute-start.1 = (f32[8,2944]{1,0:T(8,128)S(1)}, f32[8,2944]{1,0:T(8,128)S(1)}, u32[]{:S(2)}, u32[]{:S(2)}) collective-permute-start(f32[8,2944]{1,0:T(8,128)S(1)} %get-tuple-element.17), channel_id=1, source_target_pairs={{0,8},{8,16},{16,24},{24,32},{32,40},{40,48},{48,56},{56,64},{64,7... | collective-permute-start | bytes 282632 | tf_op jit(solution)/shard_map/ppermute | solution.py:461
  3.1 6.3 %collective-permute-start = (f32[8,2944]{1,0:T(8,128)S(1)}, f32[8,2944]{1,0:T(8,128)S(1)}, u32[]{:S(2)}, u32[]{:S(2)}) collective-permute-start(f32[8,2944]{1,0:T(8,128)S(1)} %get-tuple-element.16._), channel_id=1, source_target_pairs={{8,0},{16,8},{24,16},{32,24},{40,32},{48,40},{56,48},{64,56},{72,6... | collective-permute-start | bytes 282632 | tf_op jit(solution)/shard_map/ppermute | solution.py:461
  9.5 5.3 %collective-permute-start.2 = (f32[96,128]{1,0:T(8,128)S(1)}, f32[96,128]{1,0:T(8,128)S(1)}, u32[]{:S(2)}, u32[]{:S(2)}) collective-permute-start(f32[96,128]{1,0:T(8,128)S(1)} %get-tuple-element.25), channel_id=1, source_target_pairs={{1,0},{2,1},{3,2},{4,3},{5,4},{6,5},{7,6},{0,7},{9,8},{10,9},{11,1... | collective-permute-start | bytes 147464 | tf_op jit(solution)/shard_map/ppermute | solution.py:461
  12.3 4.7 %collective-permute-start.3 = (f32[96,128]{1,0:T(8,128)S(1)}, f32[96,128]{1,0:T(8,128)S(1)}, u32[]{:S(2)}, u32[]{:S(2)}) collective-permute-start(f32[96,128]{1,0:T(8,128)S(1)} %get-tuple-element.26), channel_id=1, source_target_pairs={{0,1},{1,2},{2,3},{3,4},{4,5},{5,6},{6,7},{7,0},{8,9},{9,10},{10,1... | collective-permute-start | bytes 147464 | tf_op jit(solution)/shard_map/ppermute | solution.py:461

commit v2 on v1

--- a/solution.py
+++ b/solution.py
@@ -36,6 +36,7 @@
 bf16 = jnp.bfloat16
 VMEM = pl.BlockSpec(memory_space=pltpu.VMEM)
 HBM = pl.BlockSpec(memory_space=pltpu.HBM)
+ANY = pl.BlockSpec(memory_space=pl.ANY)
 SMALL = pltpu.CompilerParams(vmem_limit_bytes=6 << 20)
 
 
@@ -47,19 +48,24 @@
     return OWN + n if g == H[PLANES[n][0]] // 8 else COFF[n] + g
 
 
-def row_pack_kernel(d1, d2, d3, d4, coarse, up, down, top, bot, sems):
+def row_pack_kernel(d1, d2, d3, d4, coarse, up, down, *scratch):
+    sources = (d1, d2, d3, d4, coarse)
+    tops, bots, sems = scratch[:5], scratch[5:10], scratch[10]
     copies = []
-    for n, (k, p) in enumerate(PLANES):
-        src = coarse if p == 3 else (d1, d2, d3, d4)[k].at[p]
-        lanes = pl.ds(ROFF[n], W[k])
-        copies.append(pltpu.make_async_copy(src.at[pl.ds(0, 8), :], top.at[:, lanes], sems.at[2 * n]))
-        copies.append(
-            pltpu.make_async_copy(src.at[pl.ds(H[k] - 8, 8), :], bot.at[:, lanes], sems.at[2 * n + 1])
-        )
+    for n, src in enumerate(sources):
+        last = src.shape[-2] - 8
+        for side, at, dst in ((0, 0, tops[n]), (1, last, bots[n])):
+            rows = src.at[pl.ds(at, 8), :] if n == 4 else src.at[:, pl.ds(at, 8), :]
+            copies.append(pltpu.make_async_copy(rows, dst, sems.at[2 * n + side]))
     for c in copies:
         c.start()
     for c in copies:
         c.wait()
+
+    def line(refs):
+        return jnp.concatenate([refs[k][p] if p < 3 else refs[4][...] for k, p in PLANES], axis=1)
+
+    top, bot = line(tops), line(bots)
     low = iota((8, HALF), 0) < 4
     up[...] = jnp.where(low, top[:, :HALF], pltpu.roll(top[:, HALF:], 4, 0))
     down[...] = jnp.where(low, pltpu.roll(bot[:, :HALF], 4, 0), bot[:, HALF:])
@@ -67,16 +73,13 @@
 
 def row_pack(coarse, details):
     out = jax.ShapeDtypeStruct((8, HALF), f32)
+    edges = [pltpu.VMEM((3, 8, w), f32) for w in W] + [pltpu.VMEM((8, W[3]), f32)]
     return pl.pallas_call(
         row_pack_kernel,
         in_specs=[HBM] * 5,
         out_specs=[VMEM] * 2,
         out_shape=[out, out],
-        scratch_shapes=[
-            pltpu.VMEM((8, RW), f32),
-            pltpu.VMEM((8, RW), f32),
-            pltpu.SemaphoreType.DMA((26,)),
-        ],
+        scratch_shapes=edges + edges + [pltpu.SemaphoreType.DMA((10,))],
         compiler_params=SMALL,
         name="row_pack",
     )(*(pltpu.with_memory_space_constraint(x, pltpu.HBM) for x in (*details, coarse)))
@@ -125,11 +128,12 @@
         right_out[8 * m : 8 * m + 8, :] = racc[m]
 
 
-def corner_kernel(left, right, after, before, left_out, right_out):
+def corner_kernel(left, right, after, before, _, across, within):
+    odd = lax.axis_index("cols") % 2 == 1
     first, second = row_unpack(after[...], before[...])
     lane = iota((8, 128), 1)
-    left_out[...] = left[...]
-    right_out[...] = right[...]
+    across[...] = jnp.where(odd, right[...], left[...])
+    within[...] = jnp.where(odd, left[...], right[...])
 
     def piece(o):
         return first[:, o : o + 128] if o < HALF else second[:, o - HALF : o - HALF + 128]
@@ -140,8 +144,8 @@
     rows = slice(8 * CORNER, 8 * CORNER + 8)
     lacc, racc = {CORNER: left[rows, :]}, {CORNER: right[rows, :]}
     place([(OWN + n, functools.partial(edge, n)) for n in range(13)], lacc, racc)
-    left_out[rows, :] = lacc[CORNER]
-    right_out[rows, :] = racc[CORNER]
+    across[rows, :] = jnp.where(odd, racc[CORNER], lacc[CORNER])
+    within[rows, :] = jnp.where(odd, lacc[CORNER], racc[CORNER])
 
 
 def col_pack(coarse, details, after_this):
@@ -156,16 +160,16 @@
     )(*details, coarse, after_this)
 
 
-def corners(left, right, after, before):
+def corners(left, right, after, before, after_this):
     out = jax.ShapeDtypeStruct((8 * PK, 128), f32)
     return pl.pallas_call(
         corner_kernel,
-        in_specs=[VMEM] * 4,
+        in_specs=[VMEM] * 4 + [ANY],
         out_specs=[VMEM] * 2,
         out_shape=[out, out],
         compiler_params=SMALL,
         name="corners",
-    )(left, right, after, before)
+    )(left, right, after, before, after_this)
 
 
 def vertical(load_s, load_r, groups, store_s, store_r, tmp):
@@ -256,12 +260,40 @@
         lax.fori_loop(0, n, lambda i, c: (f(i), c)[1], 0)
 
 
-def detail_kernel(d1, d2, d3, d4, after, before, v1, v2, v3, v4, xr, tmp):
+def early_kernel(d1, _, v1, tmp):
+    groups = H[0] // 8
+
+    def columns(b):
+        vertical(
+            lambda g: d1[0, 8 * g : 8 * g + 8, lanes_of(b)],
+            lambda g: d1[2, 8 * g : 8 * g + 8, lanes_of(b)] * (1.0 / SQ),
+            groups,
+            interleaved_store(v1.at[b], 0, -1),
+            interleaved_store(v1.at[b], 1, -1),
+            tmp,
+        )
+
+    loop(W[0] // 128, columns)
+
+
+def early_columns(d1, after_this):
+    return pl.pallas_call(
+        early_kernel,
+        in_specs=[VMEM, ANY],
+        out_specs=VMEM,
+        out_shape=jax.ShapeDtypeStruct((W[0] // 128, 2 * H[0], 128), f32),
+        scratch_shapes=[pltpu.VMEM((4, 512, 128), f32)],
+        compiler_params=SMALL,
+        name="early_columns",
+    )(d1, after_this)
+
+
+def detail_kernel(d1, d2, d3, d4, after, before, early, _, v1, v2, v3, v4, xr, tmp):
     details, vs = (d1, d2, d3, d4), (v1, v2, v3, v4)
     first, second = row_unpack(after[...], before[...])
     xr[:, :HALF] = first
     xr[:, HALF:] = second
-    for k in (3, 2, 1, 0):
+    for k in (3, 2, 1):
         def columns(b, k=k):
             def load(p, g):
                 if g == H[k] // 8:
@@ -275,31 +307,50 @@
 
         loop(W[k] // 128, columns)
 
-
-def detail_columns(details, after, before):
-    outs = [jax.ShapeDtypeStruct((W[k] // 128, 2 * H[k] + 16, 128), f32) for k in range(4)]
+    last = H[0] // 8 - 1
+    around = (last - 1, last, last + 1, 0, 1)
+
+    def load(p, b, i):
+        g = around[i]
+        if g > last:
+            return xr[:, ROFF[p] + 128 * b : ROFF[p] + 128 * b + 128]
+        return d1[p, 8 * g : 8 * g + 8, 128 * b : 128 * b + 128]
+
+    def put(b, odd):
+        def store(i, x):
+            if i in (1, 3):
+                v1[b, pl.ds(16 * around[i] + odd, 8, 2), :] = x
+
+        return store
+
+    for b in range(W[0] // 128):
+        vertical(
+            functools.partial(load, 0, b),
+            lambda i, b=b: load(2, b, i) * (1.0 / SQ),
+            5,
+            put(b, 0),
+            put(b, 1),
+            tmp.at[:, pl.ds(40 * b, 40), :],
+        )
+
+
+def detail_columns(details, after, before, early, after_this):
+    outs = [jax.ShapeDtypeStruct(early.shape, f32)]
+    outs += [jax.ShapeDtypeStruct((W[k] // 128, 2 * H[k] + 16, 128), f32) for k in (1, 2, 3)]
     outs.append(jax.ShapeDtypeStruct((8, RW), f32))
     return pl.pallas_call(
         detail_kernel,
-        in_specs=[VMEM] * 6,
+        in_specs=[VMEM] * 7 + [ANY],
         out_specs=[VMEM] * 5,
         out_shape=outs,
-        scratch_shapes=[pltpu.VMEM((4, 520, 128), f32)],
+        input_output_aliases={6: 0},
+        scratch_shapes=[pltpu.VMEM((4, 320, 128), f32)],
         compiler_params=SMALL,
         name="detail_columns",
-    )(*details, after, before)
-
-
-def horizontal(s, r):
-    n = s.shape[1]
-    s = s - lift_delta * (r + pltpu.roll(r, 1, 1))
-    r = r - lift_gamma * (s + pltpu.roll(s, n - 1, 1))
-    s = s - lift_beta * (r + pltpu.roll(r, 1, 1))
-    r = r - lift_alpha * (s + pltpu.roll(s, n - 1, 1))
-    return s, r
-
-
-def interleave(s, r, blocks, perm):
+    )(*details, after, before, early, after_this)
+
+
+def interleave(s, r, blocks, perm, parts=1):
     rows = s.shape[0]
     x = jnp.concatenate(
         [
@@ -310,24 +361,32 @@
     )
     hi = x.astype(bf16)
     lo = (x - hi.astype(f32)).astype(bf16)
-    y = jnp.dot(jnp.concatenate([hi, lo], axis=1), perm, preferred_element_type=f32)
+    x = jnp.concatenate([hi, lo], axis=1)
+    step = blocks * rows // parts // 16 * 16
+    cuts = [*range(0, step * parts, step), blocks * rows]
+    y = [
+        jnp.dot(x[i:j, :], perm[...], preferred_element_type=f32) for i, j in zip(cuts[:-1], cuts[1:])
+    ]
+    y = jnp.concatenate(y, axis=0)
     return [y[rows * b : rows * b + rows, :] for b in range(blocks)]
 
 
-CHUNK = (128, 264, 272, 144)
-SLOTS = 3
+CHUNK = (64, 88, 136, 144)
+SLOTS = 4
 
 
 def main_kernel(
-    coarse, d4, d3, d2, d1, v1, v2, v3, v4, xr, cafter, cbefore, out,
-    xc, u, vx, l3, l2, l1, perm, stage, tmp, sems,
+    coarse, d4, d3, d2, d1, v1, v2, v3, v4, xr, across, within, out,
+    xc, u, vx, l3, l2, l1, perm, s1, r1, s2, stage, tmp, sems,
 ):
     details, vs = (d1, d2, d3, d4), (v1, v2, v3, v4)
     lows = (l1, l2, l3)
     lane = iota((8, 128), 1)
 
     even = (iota((8 * PK, 128), 1) % 8) < 4
-    aft, bef = cafter[...], cbefore[...]
+    odd = lax.axis_index("cols") % 2 == 1
+    aft = jnp.where(odd, across[...], within[...])
+    bef = jnp.where(odd, within[...], across[...])
     comb = (jnp.where(even, bef, aft), jnp.where(even, aft, bef))
     keep = (lane < 4) | (lane >= 124)
     for q in range(CG):
@@ -374,58 +433,114 @@
                 tmp,
             )
 
-        loop(blocks, columns)
+        if blocks < 3:
+            for b in range(blocks):
+                columns(b)
+        else:
+            loop(blocks, columns)
         columns(blocks)
         high_columns(k, lambda p, g, load=load, blocks=blocks: load(p, g, blocks), vx, tmp)
 
-        def rows_of(at, rows, blocks=blocks, k=k):
-            at = pl.ds(at, rows)
-            s = jnp.concatenate([u[b, at, :] for b in range(blocks + 1)], axis=1)
-            r = jnp.concatenate([vs[k][b, at, :] for b in range(blocks)] + [vx[at, :]], axis=1)
-            return horizontal(s, r)
-
         rows = CHUNK[k]
+        count = 2 * h // rows if k == 0 else 16 * groups // rows
+        width = w + 128
+        kept = blocks + (k > 0)
+
+        def at_rows(i, rows=rows):
+            return pl.ds(i * rows if isinstance(i, int) else pl.multiple_of(i * rows, 8), rows)
+
+        def slot(i):
+            return i & 3
+
+        def u_rows(i, blocks=blocks):
+            return jnp.concatenate([u[b, at_rows(i), :] for b in range(blocks + 1)], axis=1)
+
+        def v_rows(i, blocks=blocks, k=k):
+            return jnp.concatenate(
+                [vs[k][b, at_rows(i), :] for b in range(blocks)] + [vx[at_rows(i), :]], axis=1
+            )
+
+        def held(ref, i, rows=rows, width=width):
+            return ref.at[slot(i), pl.ds(0, rows), pl.ds(0, width)]
+
+        def step1(i, width=width):
+            r = v_rows(i)
+            held(s1, i)[...] = u_rows(i) - lift_delta * (r + pltpu.roll(r, 1, 1))
+
+        def step2(i, width=width):
+            x = held(s1, i)[...]
+            held(r1, i)[...] = v_rows(i) - lift_gamma * (x + pltpu.roll(x, width - 1, 1))
+
+        def step3(i):
+            x = held(r1, i)[...]
+            held(s2, i)[...] = held(s1, i)[...] - lift_beta * (x + pltpu.roll(x, 1, 1))
+
+        def step4(i, k=k, rows=rows, width=width, blocks=blocks, kept=kept):
+            x = held(s2, i)[...]
+            y = held(r1, i)[...] - lift_alpha * (x + pltpu.roll(x, width - 1, 1))
+            parts = interleave(x, y, kept, perm, 2 if isinstance(i, int) else 1)
+            if k == 0:
+                for b in range(blocks):
+                    stage[i & (SLOTS - 1), :, 256 * b : 256 * b + 256] = parts[b]
+                return
+            low = lows[k - 1]
+            for b in range(blocks):
+                low[at_rows(i), 256 * b : 256 * b + 256] = parts[b]
+            left, right = parts[blocks][:, :128], parts[blocks][:, 128:]
+            low[at_rows(i), 256 * blocks : 256 * blocks + 128] = jnp.where(
+                iota((rows, 128), 1) < 64, left, right
+            )
+
+        steps = (step1, step2, step3, step4)
+
+        def turn(i, k=k, steps=steps, count=count, send=True):
+            def active(j):
+                return not isinstance(i, int) or 0 <= i - j < count
+
+            if k == 0 and active(3) and send:
+                if isinstance(i, int):
+                    copy_out(i - 3 - SLOTS, wait=True)
+                else:
+                    pl.when(i - 3 >= SLOTS)(lambda: copy_out(i - 3 - SLOTS, wait=True))
+            for j in reversed(range(4)):
+                if active(j):
+                    steps[j](i - j)
+            if k == 0 and active(3) and send:
+                copy_out(i - 3)
+
+        def copy_out(i, wait=False, rows=rows):
+            c = i & (SLOTS - 1)
+            c = pltpu.make_async_copy(stage.at[c], out.at[at_rows(i), :], sems.at[c])
+            if wait:
+                c.wait()
+            else:
+                c.start()
+
+        first, last = (3, count) if count > 6 else (0, 0)
+        for i in range(first):
+            turn(i)
+        if last > first:
+            lax.fori_loop(first, last, lambda i, c: (turn(i), c)[1], 0)
+        if k:
+            for i in range(last, count + 3):
+                turn(i)
+        else:
+            turn(count)
+            copy_out(count - 2 - SLOTS, wait=True)
+            copy_out(count - 1 - SLOTS, wait=True)
+            turn(count + 1, send=False)
+            turn(count + 2, send=False)
+            copy_out(count - 2)
+            copy_out(count - 1)
+
         if k:
             low = lows[k - 1]
-
-            def chunk(i, rows=rows, rows_of=rows_of, low=low, blocks=blocks):
-                at = i * rows if isinstance(i, int) else pl.multiple_of(i * rows, 8)
-                s, r = rows_of(at, rows)
-                parts = interleave(s, r, blocks + 1, perm[...])
-                for b in range(blocks):
-                    low[pl.ds(at, rows), 256 * b : 256 * b + 256] = parts[b]
-                left, right = parts[blocks][:, :128], parts[blocks][:, 128:]
-                low[pl.ds(at, rows), 256 * blocks : 256 * blocks + 128] = jnp.where(
-                    iota((rows, 128), 1) < 64, left, right
-                )
-
-            loop(16 * groups // rows, chunk)
             top = low[2 * h : 2 * h + 8, :]
             bottom = low[2 * h + 8 : 2 * h + 16, :]
             low[2 * h : 2 * h + 8, :] = jnp.where(iota(top.shape, 0) < 4, top, bottom)
         else:
-            def copy(i, slot, rows=rows):
-                return pltpu.make_async_copy(
-                    stage.at[slot], out.at[pl.ds(pl.multiple_of(i * rows, 8), rows), :], sems.at[slot]
-                )
-
-            def chunk(i, rows_of=rows_of, blocks=blocks, rows=rows):
-                slot = lax.rem(i, SLOTS)
-
-                @pl.when(i >= SLOTS)
-                def _():
-                    copy(i - SLOTS, slot).wait()
-
-                s, r = rows_of(pl.multiple_of(i * rows, 8), rows)
-                parts = interleave(s, r, blocks, perm[...])
-                for b in range(blocks):
-                    stage[slot, :, 256 * b : 256 * b + 256] = parts[b]
-                copy(i, slot).start()
-
-            n = 2 * h // rows
-            loop(n, chunk)
-            for i in range(n - SLOTS, n):
-                copy(i, i % SLOTS).wait()
+            for i in range(count - SLOTS, count):
+                copy_out(i, wait=True)
 
 
 def main(coarse, d4, d3, d2, d1, *rest):
@@ -442,6 +557,9 @@
             pltpu.VMEM((272, 640), f32),
             pltpu.VMEM((528, 1152), f32),
             pltpu.VMEM((512, 256), bf16),
+            pltpu.VMEM((4, 176, 1152), f32),
+            pltpu.VMEM((4, 176, 1152), f32),
+            pltpu.VMEM((4, 176, 1152), f32),
             pltpu.VMEM((SLOTS, CHUNK[0], 2048), f32),
             pltpu.VMEM((4, 520, 128), f32),
             pltpu.SemaphoreType.DMA((SLOTS,)),
@@ -454,18 +572,23 @@
 def per_device(coarse, detail4, detail3, detail2, detail1):
     details = (detail1, detail2, detail3, detail4)
 
-    def swap(to_prev, to_next, axis):
-        n = lax.axis_size(axis)
-        down = [((i + 1) % n, i) for i in range(n)]
-        up = [(i, (i + 1) % n) for i in range(n)]
-        return lax.ppermute(to_prev, axis, down), lax.ppermute(to_next, axis, up)
-
+    n = lax.axis_size("rows")
     up, down = row_pack(coarse, details)
-    rafter, rbefore = swap(up, down, "rows")
+    rbefore = lax.ppermute(down, "rows", [(i, (i + 1) % n) for i in range(n)])
+    rafter = lax.ppermute(up, "rows", [((i + 1) % n, i) for i in range(n)])
     packed = col_pack(coarse, details, up)
-    cafter, cbefore = swap(*corners(*packed, rafter, rbefore), "cols")
-    highs = detail_columns(details, rafter, rbefore)
-    return main(coarse, detail4, detail3, detail2, detail1, *highs, cafter, cbefore)
+    early = early_columns(detail1, packed[0])
+    sent = corners(*packed, rafter, rbefore, early)
+    across = exchange(sent[0], 1)
+    within = exchange(sent[1], 0)
+    highs = detail_columns(details, rafter, rbefore, early, sent[1])
+    return main(coarse, detail4, detail3, detail2, detail1, *highs, across, within)
+
+
+def exchange(x, first):
+    n = lax.axis_size("cols")
+    pairs = [((first + i) % n, (first + i + 1) % n) for i in range(0, n, 2)]
+    return lax.ppermute(x, "cols", pairs + [(j, i) for i, j in pairs])
 
 
 def solution(mesh):

time: 33.2 us -> 29.7 us (0.89); the launches traced: 33.1 us -> 29.1 us
  waiting for transfers between devices: 4.31 us -> 1.21 us
  Pallas kernels: 20.4 us -> 19.2 us
    ppermute x4, waiting for transfers between devices: 4.31 us -> 1.21 us  [the longest x2 0.98 us: exchange(): return lax.ppermute(x, 'cols', pairs + [(j, i) for i, j in pairs])]
    pallas_call x1, Pallas kernels: 16.1 us -> 14.8 us  [main(): pl.pallas_call(main_kernel, in_specs=[VMEM] * 12, out_specs=HBM, out_shap...]
    pallas_call x2 -> x3, Pallas kernels: 2.63 us -> 2.79 us  [the longest x1 1.92 us: early_columns(): pl.pallas_call(early_kernel, in_specs=[VMEM, ANY], out_specs=VMEM, out_sh...]
  transfers between devices with their start and end apart: 4 -> 4, of which waited for: 2 -> 2; matrix products, arithmetic and copies ran while one was open for 0% -> 0% of each run, Pallas kernels for 9% -> 11%
where the time goes in v2:
time: 29.7 us; the launch traced here: 29.1 us
  Pallas kernels  19.2 us (65%)
  starting transfers between devices  8.56 us (29%)
  waiting for transfers between devices  1.21 us (4%)
    pallas_call x1, Pallas kernels, main(): pl.pallas_call(main_kernel, in_specs=[VMEM] * 12, out_specs=HBM, out_shap...  14.8 us
    ppermute x1, starting transfers between devices, per_device(): rafter = lax.ppermute(up, 'rows', [((i + 1) % n, i) for i in range(n)])  3.71 us
    ppermute x2, starting transfers between devices, exchange(): return lax.ppermute(x, 'cols', pairs + [(j, i) for i, j in pairs])  3.08 us
    pallas_call x1, Pallas kernels, early_columns(): pl.pallas_call(early_kernel, in_specs=[VMEM, ANY], out_specs=VMEM, out_sh...  1.92 us
    ppermute x1, starting transfers between devices, per_device(): rbefore = lax.ppermute(down, 'rows', [(i, (i + 1) % n) for i in range(n)])  1.77 us
    pallas_call x1, Pallas kernels, row_pack(): pl.pallas_call(row_pack_kernel, in_specs=[HBM] * 5, out_specs=[VMEM] * 2,...  1.21 us
    ppermute x2, waiting for transfers between devices, exchange(): return lax.ppermute(x, 'cols', pairs + [(j, i) for i, j in pairs])  0.98 us
    pallas_call x1, Pallas kernels, detail_columns(): pl.pallas_call(detail_kernel, in_specs=[VMEM] * 7 + [ANY], out_specs=[VME...  0.79 us
  transfers between devices with their start and end apart: 4, of which 2 were waited for; matrix products, arithmetic and copies ran while one was open for 0% of the time, Pallas kernels for 11%

profile of v2, /device:TPU:0, one launch (start us, length us, event | category | flops | bytes accessed | tf_op | source)
XLA Modules:
  0.0 29.1 jit_solution(9894722754164948337)
XLA Ops:
  0.0 0.0 copy-start
  0.0 0.0 copy-start.1
  0.0 0.0 copy-start.2
  0.0 0.0 copy-start.3
  0.0 0.0 copy-start.4
  0.0 1.2 %row_pack.1 = (f32[8,2944]{1,0:T(8,128)S(1)}, f32[8,2944]{1,0:T(8,128)S(1)}) custom-call(f32[3,512,1024]{2,1,0:T(8,128)} %d1.9, f32[3,256,512]{2,1,0:T(8,128)} %d2.7, f32[3,128,256]{2,1,0:T(8,128)} %d3.7, f32[3,64,128]{2,1,0:T(8,128)} %d4.7, f32[64,128]{1,0:T(8,128)} %coarse.5), custom_call_target="tpu_custom_call" | custom-call | tf_op jit(solution)/shard_map/row_pack/pallas_call | solution.py:77
  1.2 1.8 %collective-permute-start.1 = (f32[8,2944]{1,0:T(8,128)S(1)}, f32[8,2944]{1,0:T(8,128)S(1)}, u32[]{:S(2)}, u32[]{:S(2)}) collective-permute-start(f32[8,2944]{1,0:T(8,128)S(1)} %get-tuple-element.17), channel_id=1, source_target_pairs={{0,8},{8,16},{16,24},{24,32},{32,40},{40,48},{48,56},{56,64},{64,7... | collective-permute-start | bytes 282632 | tf_op jit(solution)/shard_map/ppermute | solution.py:577
  3.0 3.7 %collective-permute-start = (f32[8,2944]{1,0:T(8,128)S(1)}, f32[8,2944]{1,0:T(8,128)S(1)}, u32[]{:S(2)}, u32[]{:S(2)}) collective-permute-start(f32[8,2944]{1,0:T(8,128)S(1)} %get-tuple-element.16._), channel_id=1, source_target_pairs={{8,0},{16,8},{24,16},{32,24},{40,32},{48,40},{56,48},{64,56},{72,6... | collective-permute-start | bytes 282632 | tf_op jit(solution)/shard_map/ppermute | solution.py:578
  6.7 0.0 copy-done
  6.7 0.0 copy-done.1
  6.7 0.0 copy-done.2
  6.7 0.0 copy-done.3
  6.7 0.0 copy-done.4
  6.7 0.4 %col_pack.1 = (f32[96,128]{1,0:T(8,128)S(1)}, f32[96,128]{1,0:T(8,128)S(1)}) custom-call(f32[3,512,1024]{2,1,0:T(8,128)S(1)} %copy-done, f32[3,256,512]{2,1,0:T(8,128)S(1)} %copy-done.1, f32[3,128,256]{2,1,0:T(8,128)S(1)} %copy-done.2, f32[3,64,128]{2,1,0:T(8,128)S(1)} %copy-done.3, f32[64,128]{1,0:T(8,128)S(1)} %copy-done.4, f32[8,2944]{1,0:T(8,128)S(1)} %get-tuple-element.16._), custom_call_target="tpu_custom_call" | custom-call | tf_op jit(solution)/shard_map/col_pack/pallas_call | solution.py:153
  7.2 1.9 %early_columns.1._.early = f32[8,1024,128]{2,1,0:T(8,128)S(1)} custom-call(f32[3,512,1024]{2,1,0:T(8,128)S(1)} %copy-done, f32[96,128]{1,0:T(8,128)S(1)} %get-tuple-element.18._.left), custom_call_target="tpu_custom_call" | custom-call | tf_op jit(solution)/shard_map/early_columns/pallas_call | solution.py:280
  9.1 0.2 collective-permute-done.1.before
  9.3 0.0 collective-permute-done.after
  9.3 0.1 corners.1
  9.4 3.1 %collective-permute-start.2 = (f32[96,128]{1,0:T(8,128)S(1)}, f32[96,128]{1,0:T(8,128)S(1)}, u32[]{:S(2)}, u32[]{:S(2)}) collective-permute-start(f32[96,128]{1,0:T(8,128)S(1)} %get-tuple-element.26), channel_id=1, source_target_pairs={{1,2},{3,4},{5,6},{7,0},{2,1},{4,3},{6,5},{0,7},{9,10},{11,12},{13... | collective-permute-start | bytes 147464 | tf_op jit(solution)/shard_map/ppermute | solution.py:591
  12.5 0.0 collective-permute-start.3
  12.5 0.8 %detail_columns.1 = (f32[8,1024,128]{2,1,0:T(8,128)S(1)}, f32[4,528,128]{2,1,0:T(8,128)S(1)}, f32[2,272,128]{2,1,0:T(8,128)S(1)}, f32[1,144,128]{2,1,0:T(8,128)S(1)}, f32[8,5888]{1,0:T(8,128)S(1)}) custom-call(f32[3,512,1024]{2,1,0:T(8,128)S(1)} %copy-done, f32[3,256,512]{2,1,0:T(8,128)S(1)} %copy-done.1, ...), custom_call_target="tpu_custom_call", output_to_operand_aliasing={{0}: (6, {})} | custom-call | tf_op jit(solution)/shard_map/detail_columns/pallas_call | solution.py:341
  13.3 1.0 %collective-permute-done.2.across = f32[96,128]{1,0:T(8,128)S(1)} collective-permute-done((f32[96,128]{1,0:T(8,128)S(1)}, f32[96,128]{1,0:T(8,128)S(1)}, u32[]{:S(2)}, u32[]{:S(2)}) %collective-permute-start.2) | collective-permute-done | bytes 49184 | tf_op jit(solution)/shard_map/ppermute | solution.py:591
  14.3 0.0 collective-permute-done.3.within
  14.3 14.8 %synthesis.1 = f32[1024,2048]{1,0:T(8,128)} custom-call(f32[64,128]{1,0:T(8,128)S(1)} %copy-done.4, f32[3,64,128]{2,1,0:T(8,128)S(1)} %copy-done.3, f32[3,128,256]{2,1,0:T(8,128)S(1)} %copy-done.2, f32[3,256,512]{2,1,0:T(8,128)S(1)} %copy-done.1, f32[3,512,1024]{2,1,0:T(8,128)S(1)} %copy-done, f32[8,1024,128]{2,1,0:T(8,128)S(1)} %get-tuple-element.21.v1, ...), custom_call_target="tpu_custom_call" | custom-call | tf_op jit(solution)/shard_map/synthesis/pallas_call | solution.py:547
Async XLA Ops:
  0.0 6.7 %copy-start = (f32[3,512,1024]{2,1,0:T(8,128)S(1)}, f32[3,512,1024]{2,1,0:T(8,128)}, u32[]{:S(2)}) copy-start(f32[3,512,1024]{2,1,0:T(8,128)} %d1.9) | copy-start | bytes 18874372
  0.0 6.7 %copy-start.1 = (f32[3,256,512]{2,1,0:T(8,128)S(1)}, f32[3,256,512]{2,1,0:T(8,128)}, u32[]{:S(2)}) copy-start(f32[3,256,512]{2,1,0:T(8,128)} %d2.7) | copy-start | bytes 4718596
  0.0 6.7 %copy-start.2 = (f32[3,128,256]{2,1,0:T(8,128)S(1)}, f32[3,128,256]{2,1,0:T(8,128)}, u32[]{:S(2)}) copy-start(f32[3,128,256]{2,1,0:T(8,128)} %d3.7) | copy-start | bytes 1179652
  0.0 6.7 %copy-start.3 = (f32[3,64,128]{2,1,0:T(8,128)S(1)}, f32[3,64,128]{2,1,0:T(8,128)}, u32[]{:S(2)}) copy-start(f32[3,64,128]{2,1,0:T(8,128)} %d4.7) | copy-start | bytes 294916
  0.0 6.7 %copy-start.4 = (f32[64,128]{1,0:T(8,128)S(1)}, f32[64,128]{1,0:T(8,128)}, u32[]{:S(2)}) copy-start(f32[64,128]{1,0:T(8,128)} %coarse.5) | copy-start | bytes 98308
  1.2 8.1 %collective-permute-start.1 = (f32[8,2944]{1,0:T(8,128)S(1)}, f32[8,2944]{1,0:T(8,128)S(1)}, u32[]{:S(2)}, u32[]{:S(2)}) collective-permute-start(f32[8,2944]{1,0:T(8,128)S(1)} %get-tuple-element.17), channel_id=1, source_target_pairs={{0,8},{8,16},{16,24},{24,32},{32,40},{40,48},{48,56},{56,64},{64,7... | collective-permute-start | bytes 282632 | tf_op jit(solution)/shard_map/ppermute | solution.py:577
  3.0 6.3 %collective-permute-start = (f32[8,2944]{1,0:T(8,128)S(1)}, f32[8,2944]{1,0:T(8,128)S(1)}, u32[]{:S(2)}, u32[]{:S(2)}) collective-permute-start(f32[8,2944]{1,0:T(8,128)S(1)} %get-tuple-element.16._), channel_id=1, source_target_pairs={{8,0},{16,8},{24,16},{32,24},{40,32},{48,40},{56,48},{64,56},{72,6... | collective-permute-start | bytes 282632 | tf_op jit(solution)/shard_map/ppermute | solution.py:578
  9.4 4.8 %collective-permute-start.2 = (f32[96,128]{1,0:T(8,128)S(1)}, f32[96,128]{1,0:T(8,128)S(1)}, u32[]{:S(2)}, u32[]{:S(2)}) collective-permute-start(f32[96,128]{1,0:T(8,128)S(1)} %get-tuple-element.26), channel_id=1, source_target_pairs={{1,2},{3,4},{5,6},{7,0},{2,1},{4,3},{6,5},{0,7},{9,10},{11,12},{13... | collective-permute-start | bytes 147464 | tf_op jit(solution)/shard_map/ppermute | solution.py:591
  12.5 1.8 %collective-permute-start.3 = (f32[96,128]{1,0:T(8,128)S(1)}, f32[96,128]{1,0:T(8,128)S(1)}, u32[]{:S(2)}, u32[]{:S(2)}) collective-permute-start(f32[96,128]{1,0:T(8,128)S(1)} %get-tuple-element.20._), channel_id=1, source_target_pairs={{0,1},{2,3},{4,5},{6,7},{1,0},{3,2},{5,4},{7,6},{8,9},{10,11},{12,... | collective-permute-start | bytes 147464 | tf_op jit(solution)/shard_map/ppermute | solution.py:591

commit v3 on v2

--- a/solution.py
+++ b/solution.py
@@ -172,7 +172,7 @@
     )(left, right, after, before, after_this)
 
 
-def vertical(load_s, load_r, groups, store_s, store_r, tmp):
+def vertical(load_s, load_r, groups, store_s, store_r):
     sub = iota((8, 128), 0)
     first, last = sub == 0, sub == 7
 
@@ -187,41 +187,22 @@
 
         return get
 
-    def kept(f, ref):
-        def make(g):
-            x = f(g)
-            ref[8 * g : 8 * g + 8, :] = x
-            return x
-
-        return cached(make)
-
-    def prev_of(x, ref):
-        def get(g):
-            a, b = x(g - 1), x(g)
-            if g:
-                return ref[8 * g - 1 : 8 * g + 7, :]
-            return jnp.where(first, pltpu.roll(a, 1, 0), pltpu.roll(b, 1, 0))
-
-        return get
-
-    def next_of(x, ref):
-        def get(g):
-            a, b = x(g), x(g + 1)
-            if g < groups - 1:
-                return ref[8 * g + 1 : 8 * g + 9, :]
-            return jnp.where(last, pltpu.roll(b, 7, 0), pltpu.roll(a, 7, 0))
-
-        return get
-
-    s = cached(load_s)
-    r = kept(load_r, tmp.at[0])
-    rp = prev_of(r, tmp.at[0])
-    s1 = kept(lambda g: s(g) - lift_delta * (r(g) + rp(g)), tmp.at[1])
-    s1n = next_of(s1, tmp.at[1])
-    r1 = kept(lambda g: r(g) - lift_gamma * (s1(g) + s1n(g)), tmp.at[2])
-    r1p = prev_of(r1, tmp.at[2])
-    s2 = kept(lambda g: s1(g) - lift_beta * (r1(g) + r1p(g)), tmp.at[3])
-    s2n = next_of(s2, tmp.at[3])
+    def prev_of(x):
+        turned = cached(lambda g: pltpu.roll(x(g), 1, 0))
+        return lambda g: jnp.where(first, turned(g - 1), turned(g))
+
+    def next_of(x):
+        turned = cached(lambda g: pltpu.roll(x(g), 7, 0))
+        return lambda g: jnp.where(last, turned(g + 1), turned(g))
+
+    s, r = cached(load_s), cached(load_r)
+    rp = prev_of(r)
+    s1 = cached(lambda g: s(g) - lift_delta * (r(g) + rp(g)))
+    s1n = next_of(s1)
+    r1 = cached(lambda g: r(g) - lift_gamma * (s1(g) + s1n(g)))
+    r1p = prev_of(r1)
+    s2 = cached(lambda g: s1(g) - lift_beta * (r1(g) + r1p(g)))
+    s2n = next_of(s2)
     r2 = cached(lambda g: r1(g) - lift_alpha * (s2(g) + s2n(g)))
     for g in range(groups):
         store_s(g, s2(g))
@@ -240,7 +221,7 @@
     return put
 
 
-def high_columns(k, load, ref, tmp):
+def high_columns(k, load, ref):
     groups = H[k] // 8 + 1
     skip = groups - 1 if k == 0 else -1
     vertical(
@@ -249,7 +230,6 @@
         groups,
         interleaved_store(ref, 0, skip),
         interleaved_store(ref, 1, skip),
-        tmp,
     )
 
 
@@ -260,7 +240,7 @@
         lax.fori_loop(0, n, lambda i, c: (f(i), c)[1], 0)
 
 
-def early_kernel(d1, _, v1, tmp):
+def early_kernel(d1, _, v1):
     groups = H[0] // 8
 
     def columns(b):
@@ -270,7 +250,6 @@
             groups,
             interleaved_store(v1.at[b], 0, -1),
             interleaved_store(v1.at[b], 1, -1),
-            tmp,
         )
 
     loop(W[0] // 128, columns)
@@ -282,13 +261,12 @@
         in_specs=[VMEM, ANY],
         out_specs=VMEM,
         out_shape=jax.ShapeDtypeStruct((W[0] // 128, 2 * H[0], 128), f32),
-        scratch_shapes=[pltpu.VMEM((4, 512, 128), f32)],
         compiler_params=SMALL,
         name="early_columns",
     )(d1, after_this)
 
 
-def detail_kernel(d1, d2, d3, d4, after, before, early, _, v1, v2, v3, v4, xr, tmp):
+def detail_kernel(d1, d2, d3, d4, after, before, early, _, v1, v2, v3, v4, xr):
     details, vs = (d1, d2, d3, d4), (v1, v2, v3, v4)
     first, second = row_unpack(after[...], before[...])
     xr[:, :HALF] = first
@@ -303,7 +281,7 @@
                     return xr[:, pl.ds(pl.multiple_of(o + b * 128, 128), 128)]
                 return details[k][p, 8 * g : 8 * g + 8, lanes_of(b)]
 
-            high_columns(k, load, vs[k].at[b], tmp)
+            high_columns(k, load, vs[k].at[b])
 
         loop(W[k] // 128, columns)
 
@@ -330,7 +308,6 @@
             5,
             put(b, 0),
             put(b, 1),
-            tmp.at[:, pl.ds(40 * b, 40), :],
         )
 
 
@@ -344,7 +321,6 @@
         out_specs=[VMEM] * 5,
         out_shape=outs,
         input_output_aliases={6: 0},
-        scratch_shapes=[pltpu.VMEM((4, 320, 128), f32)],
         compiler_params=SMALL,
         name="detail_columns",
     )(*details, after, before, early, after_this)
@@ -371,13 +347,13 @@
     return [y[rows * b : rows * b + rows, :] for b in range(blocks)]
 
 
-CHUNK = (64, 88, 136, 144)
+CHUNK = (128, 88, 136, 144)
 SLOTS = 4
 
 
 def main_kernel(
     coarse, d4, d3, d2, d1, v1, v2, v3, v4, xr, across, within, out,
-    xc, u, vx, l3, l2, l1, perm, s1, r1, s2, stage, tmp, sems,
+    comb, u, vx, l3, l2, l1, perm, s1, r1, s2, stage, sems,
 ):
     details, vs = (d1, d2, d3, d4), (v1, v2, v3, v4)
     lows = (l1, l2, l3)
@@ -387,15 +363,17 @@
     odd = lax.axis_index("cols") % 2 == 1
     aft = jnp.where(odd, across[...], within[...])
     bef = jnp.where(odd, within[...], across[...])
-    comb = (jnp.where(even, bef, aft), jnp.where(even, aft, bef))
+    comb[0] = jnp.where(even, bef, aft)
+    comb[1] = jnp.where(even, aft, bef)
     keep = (lane < 4) | (lane >= 124)
-    for q in range(CG):
+
+    def halo_column(q):
         m, j = divmod(q, 32)
-        t = comb[j % 2][8 * m : 8 * m + 8, :]
+        t = comb[j % 2, 8 * m : 8 * m + 8, :]
         shift = (124 - 4 * j) % 128
         if shift:
             t = pltpu.roll(t, shift, 1)
-        xc[8 * q : 8 * q + 8, :] = jnp.where(keep, t, 0.0)
+        return jnp.where(keep, t, 0.0)
 
     row = iota((512, 256), 0) % 256
     col = iota((512, 256), 1)
@@ -413,8 +391,7 @@
             if p == 3 and k < 3:
                 return lows[k][rows, lanes_of(b)]
             if isinstance(b, int) and b == blocks:
-                q = col_group(n, g)
-                return xc[8 * q : 8 * q + 8, :]
+                return halo_column(col_group(n, g))
             if g == groups - 1:
                 if isinstance(b, int):
                     return xr[:, ROFF[n] + 128 * b : ROFF[n] + 128 * b + 128]
@@ -430,7 +407,6 @@
                 groups,
                 interleaved_store(u.at[b], 0, skip),
                 interleaved_store(u.at[b], 1, skip),
-                tmp,
             )
 
         if blocks < 3:
@@ -439,7 +415,7 @@
         else:
             loop(blocks, columns)
         columns(blocks)
-        high_columns(k, lambda p, g, load=load, blocks=blocks: load(p, g, blocks), vx, tmp)
+        high_columns(k, lambda p, g, load=load, blocks=blocks: load(p, g, blocks), vx)
 
         rows = CHUNK[k]
         count = 2 * h // rows if k == 0 else 16 * groups // rows
@@ -550,7 +526,7 @@
         out_specs=HBM,
         out_shape=jax.ShapeDtypeStruct((1024, 2048), f32),
         scratch_shapes=[
-            pltpu.VMEM((8 * CG, 128), f32),
+            pltpu.VMEM((2, 8 * PK, 128), f32),
             pltpu.VMEM((9, 1040, 128), f32),
             pltpu.VMEM((1040, 128), f32),
             pltpu.VMEM((144, 384), f32),
@@ -561,7 +537,6 @@
             pltpu.VMEM((4, 176, 1152), f32),
             pltpu.VMEM((4, 176, 1152), f32),
             pltpu.VMEM((SLOTS, CHUNK[0], 2048), f32),
-            pltpu.VMEM((4, 520, 128), f32),
             pltpu.SemaphoreType.DMA((SLOTS,)),
         ],
         compiler_params=pltpu.CompilerParams(vmem_limit_bytes=32 << 20),

time: 29.7 us -> 28.6 us (0.963)
  Pallas kernels: 19.2 us -> 17.9 us
  waiting for transfers between devices: 1.21 us -> 1.91 us
    pallas_call x1, Pallas kernels: 14.8 us -> 13.9 us  [main(): pl.pallas_call(main_kernel, in_specs=[VMEM] * 12, out_specs=HBM, out_shap...]
    ppermute x1, waiting for transfers between devices: 0.22 us -> 0.62 us  [per_device(): rbefore = lax.ppermute(down, 'rows', [(i, (i + 1) % n) for i in range(n)])]
    pallas_call x1, Pallas kernels: 1.92 us -> 1.51 us  [early_columns(): pl.pallas_call(early_kernel, in_specs=[VMEM, ANY], out_specs=VMEM, out_sh...]
    ppermute x2, waiting for transfers between devices: 0.98 us -> 1.29 us  [exchange(): return lax.ppermute(x, 'cols', pairs + [(j, i) for i, j in pairs])]
  transfers between devices with their start and end apart: 4 -> 4, of which waited for: 2 -> 2; matrix products, arithmetic and copies ran while one was open for 0% -> 0% of each run, Pallas kernels for 11% -> 9%
where the time goes in v3:
time: 28.6 us; the launch traced here: 28.2 us
  Pallas kernels  17.9 us (63%)
  starting transfers between devices  8.34 us (29%)
  waiting for transfers between devices  1.91 us (7%)
    pallas_call x1, Pallas kernels, main(): pl.pallas_call(main_kernel, in_specs=[VMEM] * 12, out_specs=HBM, out_shap...  13.9 us
    ppermute x1, starting transfers between devices, per_device(): rafter = lax.ppermute(up, 'rows', [((i + 1) % n, i) for i in range(n)])  3.71 us
    ppermute x2, starting transfers between devices, exchange(): return lax.ppermute(x, 'cols', pairs + [(j, i) for i, j in pairs])  2.85 us
    ppermute x1, starting transfers between devices, per_device(): rbefore = lax.ppermute(down, 'rows', [(i, (i + 1) % n) for i in range(n)])  1.77 us
    pallas_call x1, Pallas kernels, early_columns(): pl.pallas_call(early_kernel, in_specs=[VMEM, ANY], out_specs=VMEM, out_sh...  1.51 us
    ppermute x2, waiting for transfers between devices, exchange(): return lax.ppermute(x, 'cols', pairs + [(j, i) for i, j in pairs])  1.29 us
    pallas_call x1, Pallas kernels, row_pack(): pl.pallas_call(row_pack_kernel, in_specs=[HBM] * 5, out_specs=[VMEM] * 2,...  1.21 us
    pallas_call x1, Pallas kernels, detail_columns(): pl.pallas_call(detail_kernel, in_specs=[VMEM] * 7 + [ANY], out_specs=[VME...  0.66 us
  transfers between devices with their start and end apart: 4, of which 2 were waited for; matrix products, arithmetic and copies ran while one was open for 0% of the time, Pallas kernels for 9%

profile of v3, /device:TPU:0, one launch (start us, length us, event | category | flops | bytes accessed | tf_op | source)
XLA Modules:
  0.0 28.2 jit_solution(5175933176285647364)
XLA Ops:
  0.0 0.0 copy-start
  0.0 0.0 copy-start.1
  0.0 0.0 copy-start.2
  0.0 0.0 copy-start.3
  0.0 0.0 copy-start.4
  0.0 1.2 %row_pack.1 = (f32[8,2944]{1,0:T(8,128)S(1)}, f32[8,2944]{1,0:T(8,128)S(1)}) custom-call(f32[3,512,1024]{2,1,0:T(8,128)} %d1.9, f32[3,256,512]{2,1,0:T(8,128)} %d2.7, f32[3,128,256]{2,1,0:T(8,128)} %d3.7, f32[3,64,128]{2,1,0:T(8,128)} %d4.7, f32[64,128]{1,0:T(8,128)} %coarse.5), custom_call_target="tpu_custom_call" | custom-call | tf_op jit(solution)/shard_map/row_pack/pallas_call | solution.py:77
  1.2 1.8 %collective-permute-start.1 = (f32[8,2944]{1,0:T(8,128)S(1)}, f32[8,2944]{1,0:T(8,128)S(1)}, u32[]{:S(2)}, u32[]{:S(2)}) collective-permute-start(f32[8,2944]{1,0:T(8,128)S(1)} %get-tuple-element.17), channel_id=1, source_target_pairs={{0,8},{8,16},{16,24},{24,32},{32,40},{40,48},{48,56},{56,64},{64,7... | collective-permute-start | bytes 282632 | tf_op jit(solution)/shard_map/ppermute | solution.py:552
  3.0 3.7 %collective-permute-start = (f32[8,2944]{1,0:T(8,128)S(1)}, f32[8,2944]{1,0:T(8,128)S(1)}, u32[]{:S(2)}, u32[]{:S(2)}) collective-permute-start(f32[8,2944]{1,0:T(8,128)S(1)} %get-tuple-element.16._), channel_id=1, source_target_pairs={{8,0},{16,8},{24,16},{32,24},{40,32},{48,40},{56,48},{64,56},{72,6... | collective-permute-start | bytes 282632 | tf_op jit(solution)/shard_map/ppermute | solution.py:553
  6.7 0.0 copy-done
  6.7 0.0 copy-done.1
  6.7 0.0 copy-done.2
  6.7 0.0 copy-done.3
  6.7 0.0 copy-done.4
  6.7 0.4 %col_pack.1 = (f32[96,128]{1,0:T(8,128)S(1)}, f32[96,128]{1,0:T(8,128)S(1)}) custom-call(f32[3,512,1024]{2,1,0:T(8,128)S(1)} %copy-done, f32[3,256,512]{2,1,0:T(8,128)S(1)} %copy-done.1, f32[3,128,256]{2,1,0:T(8,128)S(1)} %copy-done.2, f32[3,64,128]{2,1,0:T(8,128)S(1)} %copy-done.3, f32[64,128]{1,0:T(8,128)S(1)} %copy-done.4, f32[8,2944]{1,0:T(8,128)S(1)} %get-tuple-element.16._), custom_call_target="tpu_custom_call" | custom-call | tf_op jit(solution)/shard_map/col_pack/pallas_call | solution.py:153
  7.2 1.5 %early_columns.1._.early = f32[8,1024,128]{2,1,0:T(8,128)S(1)} custom-call(f32[3,512,1024]{2,1,0:T(8,128)S(1)} %copy-done, f32[96,128]{1,0:T(8,128)S(1)} %get-tuple-element.18._.left), custom_call_target="tpu_custom_call" | custom-call | tf_op jit(solution)/shard_map/early_columns/pallas_call | solution.py:259
  8.7 0.6 %collective-permute-done.1.before = f32[8,2944]{1,0:T(8,128)S(1)} collective-permute-done((f32[8,2944]{1,0:T(8,128)S(1)}, f32[8,2944]{1,0:T(8,128)S(1)}, u32[]{:S(2)}, u32[]{:S(2)}) %collective-permute-start.1) | collective-permute-done | bytes 94240 | tf_op jit(solution)/shard_map/ppermute | solution.py:552
  9.3 0.0 collective-permute-done.after
  9.3 0.1 corners.1
  9.4 2.8 %collective-permute-start.2 = (f32[96,128]{1,0:T(8,128)S(1)}, f32[96,128]{1,0:T(8,128)S(1)}, u32[]{:S(2)}, u32[]{:S(2)}) collective-permute-start(f32[96,128]{1,0:T(8,128)S(1)} %get-tuple-element.26), channel_id=1, source_target_pairs={{1,2},{3,4},{5,6},{7,0},{2,1},{4,3},{6,5},{0,7},{9,10},{11,12},{13... | collective-permute-start | bytes 147464 | tf_op jit(solution)/shard_map/ppermute | solution.py:566
  12.3 0.0 collective-permute-start.3
  12.3 0.7 %detail_columns.1 = (f32[8,1024,128]{2,1,0:T(8,128)S(1)}, f32[4,528,128]{2,1,0:T(8,128)S(1)}, f32[2,272,128]{2,1,0:T(8,128)S(1)}, f32[1,144,128]{2,1,0:T(8,128)S(1)}, f32[8,5888]{1,0:T(8,128)S(1)}) custom-call(f32[3,512,1024]{2,1,0:T(8,128)S(1)} %copy-done, f32[3,256,512]{2,1,0:T(8,128)S(1)} %copy-done.1, ...), custom_call_target="tpu_custom_call", output_to_operand_aliasing={{0}: (6, {})} | custom-call | tf_op jit(solution)/shard_map/detail_columns/pallas_call | solution.py:318
  13.0 1.3 %collective-permute-done.2.across = f32[96,128]{1,0:T(8,128)S(1)} collective-permute-done((f32[96,128]{1,0:T(8,128)S(1)}, f32[96,128]{1,0:T(8,128)S(1)}, u32[]{:S(2)}, u32[]{:S(2)}) %collective-permute-start.2) | collective-permute-done | bytes 49184 | tf_op jit(solution)/shard_map/ppermute | solution.py:566
  14.3 0.0 collective-permute-done.3.within
  14.3 13.9 %synthesis.1 = f32[1024,2048]{1,0:T(8,128)} custom-call(f32[64,128]{1,0:T(8,128)S(1)} %copy-done.4, f32[3,64,128]{2,1,0:T(8,128)S(1)} %copy-done.3, f32[3,128,256]{2,1,0:T(8,128)S(1)} %copy-done.2, f32[3,256,512]{2,1,0:T(8,128)S(1)} %copy-done.1, f32[3,512,1024]{2,1,0:T(8,128)S(1)} %copy-done, f32[8,1024,128]{2,1,0:T(8,128)S(1)} %get-tuple-element.21.v1, ...), custom_call_target="tpu_custom_call" | custom-call | tf_op jit(solution)/shard_map/synthesis/pallas_call | solution.py:523
Async XLA Ops:
  0.0 6.7 %copy-start = (f32[3,512,1024]{2,1,0:T(8,128)S(1)}, f32[3,512,1024]{2,1,0:T(8,128)}, u32[]{:S(2)}) copy-start(f32[3,512,1024]{2,1,0:T(8,128)} %d1.9) | copy-start | bytes 18874372
  0.0 6.7 %copy-start.1 = (f32[3,256,512]{2,1,0:T(8,128)S(1)}, f32[3,256,512]{2,1,0:T(8,128)}, u32[]{:S(2)}) copy-start(f32[3,256,512]{2,1,0:T(8,128)} %d2.7) | copy-start | bytes 4718596
  0.0 6.7 %copy-start.2 = (f32[3,128,256]{2,1,0:T(8,128)S(1)}, f32[3,128,256]{2,1,0:T(8,128)}, u32[]{:S(2)}) copy-start(f32[3,128,256]{2,1,0:T(8,128)} %d3.7) | copy-start | bytes 1179652
  0.0 6.7 %copy-start.3 = (f32[3,64,128]{2,1,0:T(8,128)S(1)}, f32[3,64,128]{2,1,0:T(8,128)}, u32[]{:S(2)}) copy-start(f32[3,64,128]{2,1,0:T(8,128)} %d4.7) | copy-start | bytes 294916
  0.0 6.7 %copy-start.4 = (f32[64,128]{1,0:T(8,128)S(1)}, f32[64,128]{1,0:T(8,128)}, u32[]{:S(2)}) copy-start(f32[64,128]{1,0:T(8,128)} %coarse.5) | copy-start | bytes 98308
  1.2 8.1 %collective-permute-start.1 = (f32[8,2944]{1,0:T(8,128)S(1)}, f32[8,2944]{1,0:T(8,128)S(1)}, u32[]{:S(2)}, u32[]{:S(2)}) collective-permute-start(f32[8,2944]{1,0:T(8,128)S(1)} %get-tuple-element.17), channel_id=1, source_target_pairs={{0,8},{8,16},{16,24},{24,32},{32,40},{40,48},{48,56},{56,64},{64,7... | collective-permute-start | bytes 282632 | tf_op jit(solution)/shard_map/ppermute | solution.py:552
  3.0 6.3 %collective-permute-start = (f32[8,2944]{1,0:T(8,128)S(1)}, f32[8,2944]{1,0:T(8,128)S(1)}, u32[]{:S(2)}, u32[]{:S(2)}) collective-permute-start(f32[8,2944]{1,0:T(8,128)S(1)} %get-tuple-element.16._), channel_id=1, source_target_pairs={{8,0},{16,8},{24,16},{32,24},{40,32},{48,40},{56,48},{64,56},{72,6... | collective-permute-start | bytes 282632 | tf_op jit(solution)/shard_map/ppermute | solution.py:553
  9.4 4.8 %collective-permute-start.2 = (f32[96,128]{1,0:T(8,128)S(1)}, f32[96,128]{1,0:T(8,128)S(1)}, u32[]{:S(2)}, u32[]{:S(2)}) collective-permute-start(f32[96,128]{1,0:T(8,128)S(1)} %get-tuple-element.26), channel_id=1, source_target_pairs={{1,2},{3,4},{5,6},{7,0},{2,1},{4,3},{6,5},{0,7},{9,10},{11,12},{13... | collective-permute-start | bytes 147464 | tf_op jit(solution)/shard_map/ppermute | solution.py:566
  12.3 2.0 %collective-permute-start.3 = (f32[96,128]{1,0:T(8,128)S(1)}, f32[96,128]{1,0:T(8,128)S(1)}, u32[]{:S(2)}, u32[]{:S(2)}) collective-permute-start(f32[96,128]{1,0:T(8,128)S(1)} %get-tuple-element.20._), channel_id=1, source_target_pairs={{0,1},{2,3},{4,5},{6,7},{1,0},{3,2},{5,4},{7,6},{8,9},{10,11},{12,... | collective-permute-start | bytes 147464 | tf_op jit(solution)/shard_map/ppermute | solution.py:566

commit v4 on v3

--- a/solution.py
+++ b/solution.py
@@ -266,7 +266,11 @@
     )(d1, after_this)
 
 
-def detail_kernel(d1, d2, d3, d4, after, before, early, _, v1, v2, v3, v4, xr):
+def detail_kernel(d1, d2, d3, d4, after, before, early, _, v1, v2, v3, v4, xr, perm):
+    row = iota((512, 256), 0) % 256
+    col = iota((512, 256), 1)
+    target = jnp.where(row < 128, 2 * row, 2 * row - 255)
+    perm[...] = jnp.where(col == target, 1.0, 0.0).astype(bf16)
     details, vs = (d1, d2, d3, d4), (v1, v2, v3, v4)
     first, second = row_unpack(after[...], before[...])
     xr[:, :HALF] = first
@@ -315,10 +319,11 @@
     outs = [jax.ShapeDtypeStruct(early.shape, f32)]
     outs += [jax.ShapeDtypeStruct((W[k] // 128, 2 * H[k] + 16, 128), f32) for k in (1, 2, 3)]
     outs.append(jax.ShapeDtypeStruct((8, RW), f32))
+    outs.append(jax.ShapeDtypeStruct((512, 256), bf16))
     return pl.pallas_call(
         detail_kernel,
         in_specs=[VMEM] * 7 + [ANY],
-        out_specs=[VMEM] * 5,
+        out_specs=[VMEM] * 6,
         out_shape=outs,
         input_output_aliases={6: 0},
         compiler_params=SMALL,
@@ -326,7 +331,7 @@
     )(*details, after, before, early, after_this)
 
 
-def interleave(s, r, blocks, perm, parts=1):
+def interleave(s, r, blocks, perm, parts=2):
     rows = s.shape[0]
     x = jnp.concatenate(
         [
@@ -352,8 +357,8 @@
 
 
 def main_kernel(
-    coarse, d4, d3, d2, d1, v1, v2, v3, v4, xr, across, within, out,
-    comb, u, vx, l3, l2, l1, perm, s1, r1, s2, stage, sems,
+    coarse, d4, d3, d2, d1, v1, v2, v3, v4, xr, perm, across, within, out,
+    comb, u, vx, l3, l2, l1, s1, r1, s2, stage, sems,
 ):
     details, vs = (d1, d2, d3, d4), (v1, v2, v3, v4)
     lows = (l1, l2, l3)
@@ -374,11 +379,6 @@
         if shift:
             t = pltpu.roll(t, shift, 1)
         return jnp.where(keep, t, 0.0)
-
-    row = iota((512, 256), 0) % 256
-    col = iota((512, 256), 1)
-    target = jnp.where(row < 128, 2 * row, 2 * row - 255)
-    perm[...] = jnp.where(col == target, 1.0, 0.0).astype(bf16)
 
     for k in (3, 2, 1, 0):
         h, w = H[k], W[k]
@@ -454,7 +454,7 @@
         def step4(i, k=k, rows=rows, width=width, blocks=blocks, kept=kept):
             x = held(s2, i)[...]
             y = held(r1, i)[...] - lift_alpha * (x + pltpu.roll(x, width - 1, 1))
-            parts = interleave(x, y, kept, perm, 2 if isinstance(i, int) else 1)
+            parts = interleave(x, y, kept, perm)
             if k == 0:
                 for b in range(blocks):
                     stage[i & (SLOTS - 1), :, 256 * b : 256 * b + 256] = parts[b]
@@ -522,7 +522,7 @@
 def main(coarse, d4, d3, d2, d1, *rest):
     return pl.pallas_call(
         main_kernel,
-        in_specs=[VMEM] * 12,
+        in_specs=[VMEM] * 13,
         out_specs=HBM,
         out_shape=jax.ShapeDtypeStruct((1024, 2048), f32),
         scratch_shapes=[
@@ -532,7 +532,6 @@
             pltpu.VMEM((144, 384), f32),
             pltpu.VMEM((272, 640), f32),
             pltpu.VMEM((528, 1152), f32),
-            pltpu.VMEM((512, 256), bf16),
             pltpu.VMEM((4, 176, 1152), f32),
             pltpu.VMEM((4, 176, 1152), f32),
             pltpu.VMEM((4, 176, 1152), f32),

time: 28.6 us -> 28.3 us (0.990)
    pallas_call x1, Pallas kernels: 13.9 us -> 13.6 us  [main(): pl.pallas_call(main_kernel, in_specs=[VMEM] * 13, out_specs=HBM, out_shap...]
  transfers between devices with their start and end apart: 4 -> 4, of which waited for: 2 -> 2; matrix products, arithmetic and copies ran while one was open for 0% -> 0% of each run, Pallas kernels for 9% -> 10%
where the time goes in v4:
time: 28.3 us; the launch traced here: 27.9 us
  Pallas kernels  17.7 us (63%)
  starting transfers between devices  8.34 us (29%)
  waiting for transfers between devices  1.79 us (6%)
    pallas_call x1, Pallas kernels, main(): pl.pallas_call(main_kernel, in_specs=[VMEM] * 13, out_specs=HBM, out_shap...  13.6 us
    ppermute x1, starting transfers between devices, per_device(): rafter = lax.ppermute(up, 'rows', [((i + 1) % n, i) for i in range(n)])  3.71 us
    ppermute x2, starting transfers between devices, exchange(): return lax.ppermute(x, 'cols', pairs + [(j, i) for i, j in pairs])  2.85 us
    ppermute x1, starting transfers between devices, per_device(): rbefore = lax.ppermute(down, 'rows', [(i, (i + 1) % n) for i in range(n)])  1.77 us
    pallas_call x1, Pallas kernels, early_columns(): pl.pallas_call(early_kernel, in_specs=[VMEM, ANY], out_specs=VMEM, out_sh...  1.51 us
    pallas_call x1, Pallas kernels, row_pack(): pl.pallas_call(row_pack_kernel, in_specs=[HBM] * 5, out_specs=[VMEM] * 2,...  1.21 us
    ppermute x2, waiting for transfers between devices, exchange(): return lax.ppermute(x, 'cols', pairs + [(j, i) for i, j in pairs])  1.17 us
    pallas_call x1, Pallas kernels, detail_columns(): pl.pallas_call(detail_kernel, in_specs=[VMEM] * 7 + [ANY], out_specs=[VME...  0.78 us
  transfers between devices with their start and end apart: 4, of which 2 were waited for; matrix products, arithmetic and copies ran while one was open for 0% of the time, Pallas kernels for 10%

profile of v4, /device:TPU:0, one launch (start us, length us, event | category | flops | bytes accessed | tf_op | source)
XLA Modules:
  0.0 27.9 jit_solution(17143500055479777031)
XLA Ops:
  0.0 0.0 copy-start
  0.0 0.0 copy-start.1
  0.0 0.0 copy-start.2
  0.0 0.0 copy-start.3
  0.0 0.0 copy-start.4
  0.0 1.2 %row_pack.1 = (f32[8,2944]{1,0:T(8,128)S(1)}, f32[8,2944]{1,0:T(8,128)S(1)}) custom-call(f32[3,512,1024]{2,1,0:T(8,128)} %d1.9, f32[3,256,512]{2,1,0:T(8,128)} %d2.7, f32[3,128,256]{2,1,0:T(8,128)} %d3.7, f32[3,64,128]{2,1,0:T(8,128)} %d4.7, f32[64,128]{1,0:T(8,128)} %coarse.5), custom_call_target="tpu_custom_call" | custom-call | tf_op jit(solution)/shard_map/row_pack/pallas_call | solution.py:77
  1.2 1.8 %collective-permute-start.1 = (f32[8,2944]{1,0:T(8,128)S(1)}, f32[8,2944]{1,0:T(8,128)S(1)}, u32[]{:S(2)}, u32[]{:S(2)}) collective-permute-start(f32[8,2944]{1,0:T(8,128)S(1)} %get-tuple-element.18), channel_id=1, source_target_pairs={{0,8},{8,16},{16,24},{24,32},{32,40},{40,48},{48,56},{56,64},{64,7... | collective-permute-start | bytes 282632 | tf_op jit(solution)/shard_map/ppermute | solution.py:551
  3.0 3.7 %collective-permute-start = (f32[8,2944]{1,0:T(8,128)S(1)}, f32[8,2944]{1,0:T(8,128)S(1)}, u32[]{:S(2)}, u32[]{:S(2)}) collective-permute-start(f32[8,2944]{1,0:T(8,128)S(1)} %get-tuple-element.17._), channel_id=1, source_target_pairs={{8,0},{16,8},{24,16},{32,24},{40,32},{48,40},{56,48},{64,56},{72,6... | collective-permute-start | bytes 282632 | tf_op jit(solution)/shard_map/ppermute | solution.py:552
  6.7 0.0 copy-done
  6.7 0.0 copy-done.1
  6.7 0.0 copy-done.2
  6.7 0.0 copy-done.3
  6.7 0.0 copy-done.4
  6.7 0.4 %col_pack.1 = (f32[96,128]{1,0:T(8,128)S(1)}, f32[96,128]{1,0:T(8,128)S(1)}) custom-call(f32[3,512,1024]{2,1,0:T(8,128)S(1)} %copy-done, f32[3,256,512]{2,1,0:T(8,128)S(1)} %copy-done.1, f32[3,128,256]{2,1,0:T(8,128)S(1)} %copy-done.2, f32[3,64,128]{2,1,0:T(8,128)S(1)} %copy-done.3, f32[64,128]{1,0:T(8,128)S(1)} %copy-done.4, f32[8,2944]{1,0:T(8,128)S(1)} %get-tuple-element.17._), custom_call_target="tpu_custom_call" | custom-call | tf_op jit(solution)/shard_map/col_pack/pallas_call | solution.py:153
  7.2 1.5 %early_columns.1._.early = f32[8,1024,128]{2,1,0:T(8,128)S(1)} custom-call(f32[3,512,1024]{2,1,0:T(8,128)S(1)} %copy-done, f32[96,128]{1,0:T(8,128)S(1)} %get-tuple-element.19._.left), custom_call_target="tpu_custom_call" | custom-call | tf_op jit(solution)/shard_map/early_columns/pallas_call | solution.py:259
  8.7 0.6 %collective-permute-done.1.before = f32[8,2944]{1,0:T(8,128)S(1)} collective-permute-done((f32[8,2944]{1,0:T(8,128)S(1)}, f32[8,2944]{1,0:T(8,128)S(1)}, u32[]{:S(2)}, u32[]{:S(2)}) %collective-permute-start.1) | collective-permute-done | bytes 94240 | tf_op jit(solution)/shard_map/ppermute | solution.py:551
  9.3 0.0 collective-permute-done.after
  9.3 0.1 corners.1
  9.4 2.8 %collective-permute-start.2 = (f32[96,128]{1,0:T(8,128)S(1)}, f32[96,128]{1,0:T(8,128)S(1)}, u32[]{:S(2)}, u32[]{:S(2)}) collective-permute-start(f32[96,128]{1,0:T(8,128)S(1)} %get-tuple-element.28), channel_id=1, source_target_pairs={{1,2},{3,4},{5,6},{7,0},{2,1},{4,3},{6,5},{0,7},{9,10},{11,12},{13... | collective-permute-start | bytes 147464 | tf_op jit(solution)/shard_map/ppermute | solution.py:565
  12.3 0.0 collective-permute-start.3
  12.3 0.8 %detail_columns.1 = (f32[8,1024,128]{2,1,0:T(8,128)S(1)}, f32[4,528,128]{2,1,0:T(8,128)S(1)}, f32[2,272,128]{2,1,0:T(8,128)S(1)}, f32[1,144,128]{2,1,0:T(8,128)S...) custom-call(f32[3,512,1024]{2,1,0:T(8,128)S(1)} %copy-done, ...), custom_call_target="tpu_custom_call", output_to_operand_aliasing={{0}: (6, {})} | custom-call | tf_op jit(solution)/shard_map/detail_columns/pallas_call | solution.py:323
  13.1 1.2 %collective-permute-done.2.across = f32[96,128]{1,0:T(8,128)S(1)} collective-permute-done((f32[96,128]{1,0:T(8,128)S(1)}, f32[96,128]{1,0:T(8,128)S(1)}, u32[]{:S(2)}, u32[]{:S(2)}) %collective-permute-start.2) | collective-permute-done | bytes 49184 | tf_op jit(solution)/shard_map/ppermute | solution.py:565
  14.3 0.0 collective-permute-done.3.within
  14.3 13.6 %synthesis.1 = f32[1024,2048]{1,0:T(8,128)} custom-call(f32[64,128]{1,0:T(8,128)S(1)} %copy-done.4, f32[3,64,128]{2,1,0:T(8,128)S(1)} %copy-done.3, f32[3,128,256]{2,1,0:T(8,128)S(1)} %copy-done.2, f32[3,256,512]{2,1,0:T(8,128)S(1)} %copy-done.1, f32[3,512,1024]{2,1,0:T(8,128)S(1)} %copy-done, f32[8,1024,128]{2,1,0:T(8,128)S(1)} %get-tuple-element.22.v1, ...), custom_call_target="tpu_custom_call" | custom-call | tf_op jit(solution)/shard_map/synthesis/pallas_call | solution.py:523
Async XLA Ops:
  0.0 6.7 %copy-start = (f32[3,512,1024]{2,1,0:T(8,128)S(1)}, f32[3,512,1024]{2,1,0:T(8,128)}, u32[]{:S(2)}) copy-start(f32[3,512,1024]{2,1,0:T(8,128)} %d1.9) | copy-start | bytes 18874372
  0.0 6.7 %copy-start.1 = (f32[3,256,512]{2,1,0:T(8,128)S(1)}, f32[3,256,512]{2,1,0:T(8,128)}, u32[]{:S(2)}) copy-start(f32[3,256,512]{2,1,0:T(8,128)} %d2.7) | copy-start | bytes 4718596
  0.0 6.7 %copy-start.2 = (f32[3,128,256]{2,1,0:T(8,128)S(1)}, f32[3,128,256]{2,1,0:T(8,128)}, u32[]{:S(2)}) copy-start(f32[3,128,256]{2,1,0:T(8,128)} %d3.7) | copy-start | bytes 1179652
  0.0 6.7 %copy-start.3 = (f32[3,64,128]{2,1,0:T(8,128)S(1)}, f32[3,64,128]{2,1,0:T(8,128)}, u32[]{:S(2)}) copy-start(f32[3,64,128]{2,1,0:T(8,128)} %d4.7) | copy-start | bytes 294916
  0.0 6.7 %copy-start.4 = (f32[64,128]{1,0:T(8,128)S(1)}, f32[64,128]{1,0:T(8,128)}, u32[]{:S(2)}) copy-start(f32[64,128]{1,0:T(8,128)} %coarse.5) | copy-start | bytes 98308
  1.2 8.1 %collective-permute-start.1 = (f32[8,2944]{1,0:T(8,128)S(1)}, f32[8,2944]{1,0:T(8,128)S(1)}, u32[]{:S(2)}, u32[]{:S(2)}) collective-permute-start(f32[8,2944]{1,0:T(8,128)S(1)} %get-tuple-element.18), channel_id=1, source_target_pairs={{0,8},{8,16},{16,24},{24,32},{32,40},{40,48},{48,56},{56,64},{64,7... | collective-permute-start | bytes 282632 | tf_op jit(solution)/shard_map/ppermute | solution.py:551
  3.0 6.3 %collective-permute-start = (f32[8,2944]{1,0:T(8,128)S(1)}, f32[8,2944]{1,0:T(8,128)S(1)}, u32[]{:S(2)}, u32[]{:S(2)}) collective-permute-start(f32[8,2944]{1,0:T(8,128)S(1)} %get-tuple-element.17._), channel_id=1, source_target_pairs={{8,0},{16,8},{24,16},{32,24},{40,32},{48,40},{56,48},{64,56},{72,6... | collective-permute-start | bytes 282632 | tf_op jit(solution)/shard_map/ppermute | solution.py:552
  9.4 4.8 %collective-permute-start.2 = (f32[96,128]{1,0:T(8,128)S(1)}, f32[96,128]{1,0:T(8,128)S(1)}, u32[]{:S(2)}, u32[]{:S(2)}) collective-permute-start(f32[96,128]{1,0:T(8,128)S(1)} %get-tuple-element.28), channel_id=1, source_target_pairs={{1,2},{3,4},{5,6},{7,0},{2,1},{4,3},{6,5},{0,7},{9,10},{11,12},{13... | collective-permute-start | bytes 147464 | tf_op jit(solution)/shard_map/ppermute | solution.py:565
  12.3 2.0 %collective-permute-start.3 = (f32[96,128]{1,0:T(8,128)S(1)}, f32[96,128]{1,0:T(8,128)S(1)}, u32[]{:S(2)}, u32[]{:S(2)}) collective-permute-start(f32[96,128]{1,0:T(8,128)S(1)} %get-tuple-element.21._), channel_id=1, source_target_pairs={{0,1},{2,3},{4,5},{6,7},{1,0},{3,2},{5,4},{7,6},{8,9},{10,11},{12,... | collective-permute-start | bytes 147464 | tf_op jit(solution)/shard_map/ppermute | solution.py:565

commit v5 on v4

--- a/solution.py
+++ b/solution.py
@@ -352,7 +352,7 @@
     return [y[rows * b : rows * b + rows, :] for b in range(blocks)]
 
 
-CHUNK = (128, 88, 136, 144)
+CHUNK = (128, 176, 136, 144)
 SLOTS = 4
 
 

time: 28.3 us -> 28.2 us (level)
  no operation moved by 1% of the time
where the time goes in v5:
time: 28.2 us; the launch traced here: 27.8 us
  Pallas kernels  17.6 us (62%)
  starting transfers between devices  8.34 us (30%)
  waiting for transfers between devices  1.79 us (6%)
    pallas_call x1, Pallas kernels, main(): pl.pallas_call(main_kernel, in_specs=[VMEM] * 13, out_specs=HBM, out_shap...  13.6 us
    ppermute x1, starting transfers between devices, per_device(): rafter = lax.ppermute(up, 'rows', [((i + 1) % n, i) for i in range(n)])  3.71 us
    ppermute x2, starting transfers between devices, exchange(): return lax.ppermute(x, 'cols', pairs + [(j, i) for i, j in pairs])  2.85 us
    ppermute x1, starting transfers between devices, per_device(): rbefore = lax.ppermute(down, 'rows', [(i, (i + 1) % n) for i in range(n)])  1.77 us
    pallas_call x1, Pallas kernels, early_columns(): pl.pallas_call(early_kernel, in_specs=[VMEM, ANY], out_specs=VMEM, out_sh...  1.51 us
    pallas_call x1, Pallas kernels, row_pack(): pl.pallas_call(row_pack_kernel, in_specs=[HBM] * 5, out_specs=[VMEM] * 2,...  1.21 us
    ppermute x2, waiting for transfers between devices, exchange(): return lax.ppermute(x, 'cols', pairs + [(j, i) for i, j in pairs])  1.17 us
    pallas_call x1, Pallas kernels, detail_columns(): pl.pallas_call(detail_kernel, in_specs=[VMEM] * 7 + [ANY], out_specs=[VME...  0.78 us
  transfers between devices with their start and end apart: 4, of which 2 were waited for; matrix products, arithmetic and copies ran while one was open for 0% of the time, Pallas kernels for 10%

profile of v5, /device:TPU:0, one launch (start us, length us, event | category | flops | bytes accessed | tf_op | source)
XLA Modules:
  0.0 27.8 jit_solution(9035991944015738017)
XLA Ops:
  0.0 0.0 copy-start
  0.0 0.0 copy-start.1
  0.0 0.0 copy-start.2
  0.0 0.0 copy-start.3
  0.0 0.0 copy-start.4
  0.0 1.2 %row_pack.1 = (f32[8,2944]{1,0:T(8,128)S(1)}, f32[8,2944]{1,0:T(8,128)S(1)}) custom-call(f32[3,512,1024]{2,1,0:T(8,128)} %d1.9, f32[3,256,512]{2,1,0:T(8,128)} %d2.7, f32[3,128,256]{2,1,0:T(8,128)} %d3.7, f32[3,64,128]{2,1,0:T(8,128)} %d4.7, f32[64,128]{1,0:T(8,128)} %coarse.5), custom_call_target="tpu_custom_call" | custom-call | tf_op jit(solution)/shard_map/row_pack/pallas_call | solution.py:77
  1.2 1.8 %collective-permute-start.1 = (f32[8,2944]{1,0:T(8,128)S(1)}, f32[8,2944]{1,0:T(8,128)S(1)}, u32[]{:S(2)}, u32[]{:S(2)}) collective-permute-start(f32[8,2944]{1,0:T(8,128)S(1)} %get-tuple-element.18), channel_id=1, source_target_pairs={{0,8},{8,16},{16,24},{24,32},{32,40},{40,48},{48,56},{56,64},{64,7... | collective-permute-start | bytes 282632 | tf_op jit(solution)/shard_map/ppermute | solution.py:551
  3.0 3.7 %collective-permute-start = (f32[8,2944]{1,0:T(8,128)S(1)}, f32[8,2944]{1,0:T(8,128)S(1)}, u32[]{:S(2)}, u32[]{:S(2)}) collective-permute-start(f32[8,2944]{1,0:T(8,128)S(1)} %get-tuple-element.17._), channel_id=1, source_target_pairs={{8,0},{16,8},{24,16},{32,24},{40,32},{48,40},{56,48},{64,56},{72,6... | collective-permute-start | bytes 282632 | tf_op jit(solution)/shard_map/ppermute | solution.py:552
  6.7 0.0 copy-done
  6.7 0.0 copy-done.1
  6.7 0.0 copy-done.2
  6.7 0.0 copy-done.3
  6.7 0.0 copy-done.4
  6.7 0.4 %col_pack.1 = (f32[96,128]{1,0:T(8,128)S(1)}, f32[96,128]{1,0:T(8,128)S(1)}) custom-call(f32[3,512,1024]{2,1,0:T(8,128)S(1)} %copy-done, f32[3,256,512]{2,1,0:T(8,128)S(1)} %copy-done.1, f32[3,128,256]{2,1,0:T(8,128)S(1)} %copy-done.2, f32[3,64,128]{2,1,0:T(8,128)S(1)} %copy-done.3, f32[64,128]{1,0:T(8,128)S(1)} %copy-done.4, f32[8,2944]{1,0:T(8,128)S(1)} %get-tuple-element.17._), custom_call_target="tpu_custom_call" | custom-call | tf_op jit(solution)/shard_map/col_pack/pallas_call | solution.py:153
  7.2 1.5 %early_columns.1._.early = f32[8,1024,128]{2,1,0:T(8,128)S(1)} custom-call(f32[3,512,1024]{2,1,0:T(8,128)S(1)} %copy-done, f32[96,128]{1,0:T(8,128)S(1)} %get-tuple-element.19._.left), custom_call_target="tpu_custom_call" | custom-call | tf_op jit(solution)/shard_map/early_columns/pallas_call | solution.py:259
  8.7 0.6 %collective-permute-done.1.before = f32[8,2944]{1,0:T(8,128)S(1)} collective-permute-done((f32[8,2944]{1,0:T(8,128)S(1)}, f32[8,2944]{1,0:T(8,128)S(1)}, u32[]{:S(2)}, u32[]{:S(2)}) %collective-permute-start.1) | collective-permute-done | bytes 94240 | tf_op jit(solution)/shard_map/ppermute | solution.py:551
  9.3 0.0 collective-permute-done.after
  9.3 0.1 corners.1
  9.4 2.8 %collective-permute-start.2 = (f32[96,128]{1,0:T(8,128)S(1)}, f32[96,128]{1,0:T(8,128)S(1)}, u32[]{:S(2)}, u32[]{:S(2)}) collective-permute-start(f32[96,128]{1,0:T(8,128)S(1)} %get-tuple-element.28), channel_id=1, source_target_pairs={{1,2},{3,4},{5,6},{7,0},{2,1},{4,3},{6,5},{0,7},{9,10},{11,12},{13... | collective-permute-start | bytes 147464 | tf_op jit(solution)/shard_map/ppermute | solution.py:565
  12.3 0.0 collective-permute-start.3
  12.3 0.8 %detail_columns.1 = (f32[8,1024,128]{2,1,0:T(8,128)S(1)}, f32[4,528,128]{2,1,0:T(8,128)S(1)}, f32[2,272,128]{2,1,0:T(8,128)S(1)}, f32[1,144,128]{2,1,0:T(8,128)S...) custom-call(f32[3,512,1024]{2,1,0:T(8,128)S(1)} %copy-done, ...), custom_call_target="tpu_custom_call", output_to_operand_aliasing={{0}: (6, {})} | custom-call | tf_op jit(solution)/shard_map/detail_columns/pallas_call | solution.py:323
  13.1 1.2 %collective-permute-done.2.across = f32[96,128]{1,0:T(8,128)S(1)} collective-permute-done((f32[96,128]{1,0:T(8,128)S(1)}, f32[96,128]{1,0:T(8,128)S(1)}, u32[]{:S(2)}, u32[]{:S(2)}) %collective-permute-start.2) | collective-permute-done | bytes 49184 | tf_op jit(solution)/shard_map/ppermute | solution.py:565
  14.3 0.0 collective-permute-done.3.within
  14.3 13.6 %synthesis.1 = f32[1024,2048]{1,0:T(8,128)} custom-call(f32[64,128]{1,0:T(8,128)S(1)} %copy-done.4, f32[3,64,128]{2,1,0:T(8,128)S(1)} %copy-done.3, f32[3,128,256]{2,1,0:T(8,128)S(1)} %copy-done.2, f32[3,256,512]{2,1,0:T(8,128)S(1)} %copy-done.1, f32[3,512,1024]{2,1,0:T(8,128)S(1)} %copy-done, f32[8,1024,128]{2,1,0:T(8,128)S(1)} %get-tuple-element.22.v1, ...), custom_call_target="tpu_custom_call" | custom-call | tf_op jit(solution)/shard_map/synthesis/pallas_call | solution.py:523
Async XLA Ops:
  0.0 6.7 %copy-start = (f32[3,512,1024]{2,1,0:T(8,128)S(1)}, f32[3,512,1024]{2,1,0:T(8,128)}, u32[]{:S(2)}) copy-start(f32[3,512,1024]{2,1,0:T(8,128)} %d1.9) | copy-start | bytes 18874372
  0.0 6.7 %copy-start.1 = (f32[3,256,512]{2,1,0:T(8,128)S(1)}, f32[3,256,512]{2,1,0:T(8,128)}, u32[]{:S(2)}) copy-start(f32[3,256,512]{2,1,0:T(8,128)} %d2.7) | copy-start | bytes 4718596
  0.0 6.7 %copy-start.2 = (f32[3,128,256]{2,1,0:T(8,128)S(1)}, f32[3,128,256]{2,1,0:T(8,128)}, u32[]{:S(2)}) copy-start(f32[3,128,256]{2,1,0:T(8,128)} %d3.7) | copy-start | bytes 1179652
  0.0 6.7 %copy-start.3 = (f32[3,64,128]{2,1,0:T(8,128)S(1)}, f32[3,64,128]{2,1,0:T(8,128)}, u32[]{:S(2)}) copy-start(f32[3,64,128]{2,1,0:T(8,128)} %d4.7) | copy-start | bytes 294916
  0.0 6.7 %copy-start.4 = (f32[64,128]{1,0:T(8,128)S(1)}, f32[64,128]{1,0:T(8,128)}, u32[]{:S(2)}) copy-start(f32[64,128]{1,0:T(8,128)} %coarse.5) | copy-start | bytes 98308
  1.2 8.1 %collective-permute-start.1 = (f32[8,2944]{1,0:T(8,128)S(1)}, f32[8,2944]{1,0:T(8,128)S(1)}, u32[]{:S(2)}, u32[]{:S(2)}) collective-permute-start(f32[8,2944]{1,0:T(8,128)S(1)} %get-tuple-element.18), channel_id=1, source_target_pairs={{0,8},{8,16},{16,24},{24,32},{32,40},{40,48},{48,56},{56,64},{64,7... | collective-permute-start | bytes 282632 | tf_op jit(solution)/shard_map/ppermute | solution.py:551
  3.0 6.3 %collective-permute-start = (f32[8,2944]{1,0:T(8,128)S(1)}, f32[8,2944]{1,0:T(8,128)S(1)}, u32[]{:S(2)}, u32[]{:S(2)}) collective-permute-start(f32[8,2944]{1,0:T(8,128)S(1)} %get-tuple-element.17._), channel_id=1, source_target_pairs={{8,0},{16,8},{24,16},{32,24},{40,32},{48,40},{56,48},{64,56},{72,6... | collective-permute-start | bytes 282632 | tf_op jit(solution)/shard_map/ppermute | solution.py:552
  9.4 4.8 %collective-permute-start.2 = (f32[96,128]{1,0:T(8,128)S(1)}, f32[96,128]{1,0:T(8,128)S(1)}, u32[]{:S(2)}, u32[]{:S(2)}) collective-permute-start(f32[96,128]{1,0:T(8,128)S(1)} %get-tuple-element.28), channel_id=1, source_target_pairs={{1,2},{3,4},{5,6},{7,0},{2,1},{4,3},{6,5},{0,7},{9,10},{11,12},{13... | collective-permute-start | bytes 147464 | tf_op jit(solution)/shard_map/ppermute | solution.py:565
  12.3 2.0 %collective-permute-start.3 = (f32[96,128]{1,0:T(8,128)S(1)}, f32[96,128]{1,0:T(8,128)S(1)}, u32[]{:S(2)}, u32[]{:S(2)}) collective-permute-start(f32[96,128]{1,0:T(8,128)S(1)} %get-tuple-element.21._), channel_id=1, source_target_pairs={{0,1},{2,3},{4,5},{6,7},{1,0},{3,2},{5,4},{7,6},{8,9},{10,11},{12,... | collective-permute-start | bytes 147464 | tf_op jit(solution)/shard_map/ppermute | solution.py:565
